TPU v7x, 16 devices: a whole 2x2x2 slice. The times are simulated.
16 devices in a mesh: fsdp: 16 (over z, y, x, core).
Axes of the slice: x: 2, y: 2, z: 2, core: 2. Of those that a mesh axis runs over, the one named last changes fastest.
Arguments:
- tok_ids: int32 [16, 512], P('fsdp')
- tok_labels: int32 [16, 512], P('fsdp')
- embed: bfloat16 [50304, 768], P('fsdp')
- w_gate: bfloat16 [768, 3072], P('fsdp')
- w_up: bfloat16 [768, 3072], P('fsdp')
- w_down: bfloat16 [3072, 768], P('fsdp')
- gain_mlp: float32 [768], replicated
- gain_final: float32 [768], replicated
Outputs:
- output 1: float32 [], replicated
- output 2: float32 [50304, 768], P('fsdp')
- output 3: float32 [768, 3072], P('fsdp')
- output 4: float32 [768, 3072], P('fsdp')
- output 5: float32 [3072, 768], P('fsdp')
All inputs are finite; a program needn't handle non-finite values.
Results may differ from a plain program's by a relative error of at most 0.00797805.
Values are sent between devices in bfloat16 or wider.
A program may use at most 1 GiB of HBM per device.

v0:
```python
import math
import jax
import jax.numpy as jnp
from jax import lax
from jax.sharding import PartitionSpec as P

NORM_EPS = 1e-6


def dot_plain(left_mat, right_mat):
    return lax.dot_general(left_mat, right_mat, (((1,), (0,)), ((), ())), preferred_element_type=jnp.float32)


def dot_last(left_mat, right_mat):
    return lax.dot_general(left_mat, right_mat, (((1,), (1,)), ((), ())), preferred_element_type=jnp.float32)


def dot_first(left_mat, right_mat):
    return lax.dot_general(left_mat, right_mat, (((0,), (0,)), ((), ())), preferred_element_type=jnp.float32)


def rms_apply(values, gain_vec):
    inv_rms = lax.rsqrt(jnp.mean(values * values, axis=-1, keepdims=True) + NORM_EPS)
    return (values * inv_rms * gain_vec).astype(jnp.bfloat16), inv_rms


def rms_backward(values, inv_rms, gain_vec, grad_out):
    scaled = grad_out * gain_vec
    return inv_rms * scaled - values * (inv_rms ** 3) * jnp.mean(scaled * values, axis=-1, keepdims=True)


def mlp_forward(x_emb, w_gate, w_up, w_down, gain_mlp, gain_final):
    normed, inv_first = rms_apply(x_emb, gain_mlp)
    gate = dot_plain(normed, w_gate).astype(jnp.bfloat16)
    up_val = dot_plain(normed, w_up).astype(jnp.bfloat16)
    hidden_act = (jax.nn.silu(gate.astype(jnp.float32)) * up_val.astype(jnp.float32)).astype(jnp.bfloat16)
    mlp_out = dot_plain(hidden_act, w_down).astype(jnp.bfloat16)
    hid32 = (x_emb + mlp_out.astype(jnp.float32)).astype(jnp.bfloat16).astype(jnp.float32)
    hid_norm, inv_final = rms_apply(hid32, gain_final)
    return hid_norm, (x_emb, inv_first, normed, gate, up_val, hidden_act, hid32, inv_final)


def mlp_backward(d_hid, saved, w_gate, w_up, w_down, gain_mlp, gain_final):
    x_emb, inv_first, normed, gate, up_val, hidden_act, hid32, inv_final = saved
    d_hidden = rms_backward(hid32, inv_final, gain_final, d_hid)
    d_mlp = d_hidden.astype(jnp.bfloat16)
    d_down = dot_first(hidden_act, d_mlp)
    d_act = dot_last(d_mlp, w_down)
    gate32 = gate.astype(jnp.float32)
    gate_sig = jax.nn.sigmoid(gate32)
    d_gate_pre = (d_act * up_val.astype(jnp.float32) * gate_sig * (1.0 + gate32 * (1.0 - gate_sig))).astype(jnp.bfloat16)
    d_up_pre = (d_act * gate32 * gate_sig).astype(jnp.bfloat16)
    d_gate = dot_first(normed, d_gate_pre)
    d_up = dot_first(normed, d_up_pre)
    d_normed = dot_last(d_gate_pre, w_gate) + dot_last(d_up_pre, w_up)
    d_x = (d_hidden + rms_backward(x_emb, inv_first, gain_mlp, d_normed)).astype(jnp.bfloat16)
    return d_x, d_gate, d_up, d_down


def head_forward(hid_norm, emb_chunks, lab_flat):
    chunk_rows = emb_chunks.shape[1]
    tok_count = hid_norm.shape[0]
    col_ids = jnp.arange(chunk_rows, dtype=jnp.int32)

    def chunk_step(carry, chunk_in):
        run_max, run_sum, lab_logit = carry
        chunk_emb, chunk_idx = chunk_in
        logits = dot_last(hid_norm, chunk_emb)
        label_hit = (lab_flat - chunk_idx * chunk_rows)[:, None] == col_ids[None, :]
        new_max = jnp.maximum(run_max, jnp.max(logits, axis=1))
        run_sum = run_sum * jnp.exp(run_max - new_max) + jnp.sum(jnp.exp(logits - new_max[:, None]), axis=1)
        lab_logit = lab_logit + jnp.sum(jnp.where(label_hit, logits, 0.0), axis=1)
        return (new_max, run_sum, lab_logit), None

    zero_tok = jnp.zeros((tok_count,), jnp.float32)
    start = (jnp.full((tok_count,), -jnp.inf, jnp.float32), zero_tok, zero_tok)
    chunk_ids = jnp.arange(emb_chunks.shape[0], dtype=jnp.int32)
    (run_max, run_sum, lab_logit), unused = lax.scan(chunk_step, start, (emb_chunks, chunk_ids))
    return run_max + jnp.log(run_sum), lab_logit


def head_backward(hid_norm, emb_chunks, lab_flat, log_norm, inv_count):
    chunk_rows = emb_chunks.shape[1]
    col_ids = jnp.arange(chunk_rows, dtype=jnp.int32)

    def chunk_step(d_hid, chunk_in):
        chunk_emb, chunk_idx = chunk_in
        logits = dot_last(hid_norm, chunk_emb)
        label_hit = (lab_flat - chunk_idx * chunk_rows)[:, None] == col_ids[None, :]
        prob_mat = jnp.exp(logits - log_norm[:, None])
        grad_logits = ((prob_mat - label_hit.astype(jnp.float32)) * inv_count).astype(jnp.bfloat16)
        return d_hid + dot_plain(grad_logits, chunk_emb), dot_first(grad_logits, hid_norm)

    chunk_ids = jnp.arange(emb_chunks.shape[0], dtype=jnp.int32)
    d_hid, d_head = lax.scan(chunk_step, jnp.zeros(hid_norm.shape, jnp.float32), (emb_chunks, chunk_ids))
    return d_hid, d_head.reshape(-1, hid_norm.shape[1])


def solution(mesh):
    group = mesh.shape['fsdp']

    def local_step(ids_blk, lab_blk, emb_shard, gate_shard, up_shard, down_shard, gain_mlp, gain_final):
        embed_full = lax.all_gather(emb_shard, 'fsdp', tiled=True)
        w_gate = lax.all_gather(gate_shard, 'fsdp', tiled=True)
        w_up = lax.all_gather(up_shard, 'fsdp', tiled=True)
        w_down = lax.all_gather(down_shard, 'fsdp', tiled=True)
        ids_flat = ids_blk.reshape(-1)
        lab_flat = lab_blk.reshape(-1)
        model_dim = embed_full.shape[1]
        emb_scale = math.sqrt(model_dim)
        inv_count = 1.0 / (ids_flat.shape[0] * group)
        x_emb = jnp.take(embed_full, ids_flat, axis=0).astype(jnp.float32) * emb_scale
        hid_norm, saved = mlp_forward(x_emb, w_gate, w_up, w_down, gain_mlp, gain_final)
        emb_chunks = embed_full.reshape(group, -1, model_dim)
        log_norm, lab_logit = head_forward(hid_norm, emb_chunks, lab_flat)
        loss = lax.psum(jnp.sum(log_norm - lab_logit), 'fsdp') * inv_count
        d_hid, d_head = head_backward(hid_norm, emb_chunks, lab_flat, log_norm, inv_count)
        d_x, d_gate, d_up, d_down = mlp_backward(d_hid, saved, w_gate, w_up, w_down, gain_mlp, gain_final)
        d_full = d_head.at[ids_flat].add(d_x.astype(jnp.float32) * emb_scale)
        d_embed = lax.psum_scatter(d_full, 'fsdp', scatter_dimension=0, tiled=True)
        d_gate = lax.psum_scatter(d_gate, 'fsdp', scatter_dimension=0, tiled=True)
        d_up = lax.psum_scatter(d_up, 'fsdp', scatter_dimension=0, tiled=True)
        d_down = lax.psum_scatter(d_down, 'fsdp', scatter_dimension=0, tiled=True)
        return loss, d_embed, d_gate, d_up, d_down

    shard_spec = P('fsdp', None)
    return jax.shard_map(local_step, mesh=mesh, in_specs=(shard_spec, shard_spec, shard_spec, shard_spec, shard_spec, shard_spec, P(), P()), out_specs=(P(), shard_spec, shard_spec, shard_spec, shard_spec), check_vma=False)
```

profile of v0, /device:TPU:0, one launch (start us, length us, event | category | flops | bytes accessed | tf_op | source)
XLA Modules:
  0.0 1921.5 jit_solution(4729661770818322019)
XLA Ops:
  10.1 277.9 %all-gather.5.cloned.1.call-done = bf16[50304,768]{1,0:T(8,128)(2,1)} async-done(((bf16[3144,768]{1,0:T(8,128)(2,1)}), bf16[50304,768]{1,0:T(8,128)(2,1)}) %all-gather.5.cloned.1.call-update) | async-done | bytes 77266960 | tf_op jit(solution)/shard_map/all_gather | solution.py:103
  293.2 33.8 %all-gather.7.cloned.1.call-done = bf16[768,3072]{1,0:T(8,128)(2,1)} async-done(((bf16[48,3072]{1,0:T(8,128)(2,1)}), bf16[768,3072]{1,0:T(8,128)(2,1)}) %all-gather.7.cloned.1.call-update) | async-done | bytes 4718608 | tf_op jit(solution)/shard_map/all_gather | solution.py:104
  327.0 6.7 convolution_convert_fusion.1
  333.6 32.3 %all-gather.9.cloned.1.call-done = bf16[768,3072]{1,0:T(8,128)(2,1)} async-done(((bf16[48,3072]{1,0:T(8,128)(2,1)}), bf16[768,3072]{1,0:T(8,128)(2,1)}) %all-gather.9.cloned.1.call-update) | async-done | bytes 4718608 | tf_op jit(solution)/shard_map/all_gather | solution.py:105
  365.9 6.6 convolution_convert_fusion
  372.5 32.1 %all-gather.11.cloned.1.call-done = bf16[3072,768]{1,0:T(8,128)(2,1)} async-done(((bf16[192,768]{1,0:T(8,128)(2,1)}), bf16[3072,768]{1,0:T(8,128)(2,1)}) %all-gather.11.cloned.1.call-update) | async-done | bytes 4718608 | tf_op jit(solution)/shard_map/all_gather | solution.py:106
  404.7 8.1 fusion.45
  413.0 205.8 %while.28 = (s32[]{:T(128)}, f32[512]{0:T(512)S(1)}, f32[512]{0:T(512)S(1)}, f32[512]{0:T(512)S(1)}, bf16[16,3144,768]{2,1,0:T(8,128)(2,1)}, /*index=5*/bf16[512...) while((s32[]{:T(128)}, f32[512]{0:T(512)S(1)}, ...), condition=%wide.region_6.7_spmd.clone, body=%wide.region_2.0_spmd.clone.sunk | while | flops 2482204160 | bytes 18535060 | solution.py:78
  413.1 7.1 fusion.94
  425.9 7.1 fusion.94
  438.8 7.1 fusion.94
  451.7 7.1 fusion.94
  464.5 7.1 fusion.94
  477.4 7.1 fusion.94
  490.2 7.1 fusion.94
  503.1 7.1 fusion.94
  516.0 7.1 fusion.94
  528.8 7.1 fusion.94
  541.7 7.1 fusion.94
  554.6 7.1 fusion.94
  567.4 7.1 fusion.94
  580.3 7.1 fusion.94
  593.2 7.1 fusion.94
  606.0 7.1 fusion.94
  619.5 324.9 %while.29 = (s32[]{:T(128)}, f32[512,768]{1,0:T(8,128)S(1)}, f32[16,3144,768]{2,1,0:T(8,128)}, bf16[16,3144,768]{2,1,0:T(8,128)(2,1)}, bf16[512,768]{1,0:T(8,128...) while((s32[]{:T(128)}, f32[512,768]{1,0:T(8,128)S(1)}, ...), condition=%wide.region_10.11_spmd.clone, body=%wide.region_9.10_spmd.clone.sunk | while | flops 7428071936 | bytes 46581420 | solution.py:95
  633.3 6.5 select_add_fusion.5
  653.6 6.5 select_add_fusion.5
  674.0 6.5 select_add_fusion.5
  694.3 6.5 select_add_fusion.5
  714.7 6.5 select_add_fusion.5
  734.9 6.5 select_add_fusion.5
  755.2 6.5 select_add_fusion.5
  775.5 6.5 select_add_fusion.5
  795.9 6.5 select_add_fusion.5
  816.2 6.5 select_add_fusion.5
  836.4 6.5 select_add_fusion.5
  856.7 6.5 select_add_fusion.5
  877.0 6.5 select_add_fusion.5
  897.3 6.5 select_add_fusion.5
  937.9 6.5 select_add_fusion.5
  944.7 10.0 fusion.51
  954.9 9.2 fusion.32
  971.1 7.2 fusion.56
  991.7 67.1 %scatter_fusion = f32[50304,768]{1,0:T(8,128)} fusion(f32[50304,768]{1,0:T(8,128)} %bitcast.5, s32[512]{0:T(512)S(1)} %bitcast.81, f32[512,768]{1,0:T(8,128)} %convert_multiply_fusion.12), kind=kCustom, calls=%fused_computation.1 | custom fusion | flops 393216 | bytes 4720640 | tf_op jit(solution)/shard_map/scatter-add | solution.py:119
  1058.9 32.6 %psum.7 = f32[]{:T(128)} all-reduce(f32[]{:T(128)} %get-tuple-element.199), channel_id=1, replica_groups=mesh['fsdp'=16] {'fsdp'}, use_global_device_ids=true, to_apply=%region_8.9 | all-reduce | flops 1 | bytes 8 | tf_op jit(solution)/shard_map/psum | solution.py:116
  1092.2 27.6 %reduce-scatter.7.cloned.1.call-done = f32[48,3072]{1,0:T(8,128)} async-done(((f32[768,3072]{1,0:T(8,128)}), f32[48,3072]{1,0:T(8,128)}) %reduce-scatter.7.cloned.1.call-update) | async-done | bytes 589840 | tf_op jit(solution)/shard_map/reduce_scatter | solution.py:121
  1119.8 84.7 %reduce-scatter.9.cloned.1.call-done = f32[48,3072]{1,0:T(8,128)} async-done(((f32[768,3072]{1,0:T(8,128)}), f32[48,3072]{1,0:T(8,128)}) %reduce-scatter.9.cloned.1.call-update) | async-done | bytes 589840 | tf_op jit(solution)/shard_map/reduce_scatter | solution.py:122
  1204.6 709.0 %reduce-scatter.13.cloned.1.call-done = f32[3144,768]{1,0:T(8,128)} async-done(((f32[50304,768]{1,0:T(8,128)}), f32[3144,768]{1,0:T(8,128)}) %reduce-scatter.13.cloned.1.call-update) | async-done | bytes 9658384
  (267 shorter events, 329.1 us)
Async XLA Ops:
  7.2 2.9 copy-start.16
  7.2 280.9 %all-gather.5.cloned.1.call-start = ((), (), s32[]{:S(2)}) async-start(), calls=%async_computation.4 | async-start | bytes 82096128 | tf_op jit(solution)/shard_map/all_gather | solution.py:103
  7.9 319.1 %all-gather.7.cloned.1.call-start = ((), (), s32[]{:S(2)}) async-start(), calls=%async_computation.5 | async-start | bytes 5013504 | tf_op jit(solution)/shard_map/all_gather | solution.py:104
  8.7 357.2 %all-gather.9.cloned.1.call-start = ((), (), s32[]{:S(2)}) async-start(), calls=%async_computation.6 | async-start | bytes 5013504 | tf_op jit(solution)/shard_map/all_gather | solution.py:105
  9.4 395.3 %all-gather.11.cloned.1.call-start = ((), (), s32[]{:S(2)}) async-start(), calls=%async_computation.7 | async-start | bytes 5013504 | tf_op jit(solution)/shard_map/all_gather | solution.py:106
  10.0 1082.2 %reduce-scatter.11.cloned.1.call-start = ((), (), s32[]{:S(2)}) async-start(), calls=%async_computation.10 | async-start | bytes 10027008 | tf_op jit(solution)/shard_map/reduce_scatter | solution.py:123
  10.1 282.0 %copy-start.12 = (s32[512,1]{0,1:T(1,128)}, s32[512,1]{0,1:T(1,128)S(1)}, u32[]{:S(2)}) copy-start(s32[512,1]{0,1:T(1,128)S(1)} %compare_select_fusion) | copy-start | bytes 6148
  10.1 394.5 %copy-start.9 = (pred[512]{0:T(512)(128)(4,1)}, pred[512]{0:T(512)(128)(4,1)S(1)}, u32[]{:S(2)}) copy-start(pred[512]{0:T(512)(128)(4,1)S(1)} %compare_and_fusion) | copy-start | bytes 1540
  10.1 316.8 %copy-start.4 = (f32[768]{0:T(1024)S(1)}, f32[768]{0:T(1024)}, u32[]{:S(2)}) copy-start(f32[768]{0:T(1024)} %param.18) | copy-start | bytes 9220
  292.1 112.5 %copy-start = (bf16[512,768]{1,0:T(8,128)(2,1)}, bf16[512,768]{1,0:T(8,128)(2,1)S(1)}, u32[]{:S(2)}) copy-start(bf16[512,768]{1,0:T(8,128)(2,1)S(1)} %gather_fusion) | copy-start | bytes 2359300
  293.2 72.7 %copy-start.6 = (f32[512]{0:T(512)}, f32[512]{0:T(512)S(1)}, u32[]{:S(2)}) copy-start(f32[512]{0:T(512)S(1)} %get-tuple-element.208) | copy-start | bytes 6148
  372.5 40.3 %copy-start.11 = (f32[768]{0:T(1024)S(1)}, f32[768]{0:T(1024)}, u32[]{:S(2)}) copy-start(f32[768]{0:T(1024)} %param.19) | copy-start | bytes 9220
  372.5 40.5 %copy-start.8 = (s32[1,512]{1,0:T(1,128)S(1)}, s32[1,512]{1,0:T(1,128)}, u32[]{:S(2)}) copy-start(s32[1,512]{1,0:T(1,128)} %param.13) | copy-start | bytes 6148
  626.5 1.7 copy-start.17
  646.8 1.7 copy-start.17
  667.1 1.7 copy-start.17
  687.5 1.7 copy-start.17
  707.8 1.7 copy-start.17
  728.2 1.7 copy-start.17
  748.4 1.7 copy-start.17
  768.7 1.7 copy-start.17
  789.0 1.7 copy-start.17
  809.4 1.7 copy-start.17
  829.7 1.7 copy-start.17
  849.9 1.7 copy-start.17
  870.2 1.7 copy-start.17
  890.5 1.7 copy-start.17
  910.8 1.7 copy-start.17
  931.2 1.7 copy-start.17
  954.8 10.9 copy-start.1
  954.8 10.9 copy-start.5
  954.8 10.9 copy-start.7
  954.8 10.8 copy-start.10
  954.8 165.0 %reduce-scatter.7.cloned.1.call-start = ((), (), s32[]{:S(2)}) async-start(), calls=%async_computation.8 | async-start | bytes 10027008 | tf_op jit(solution)/shard_map/reduce_scatter | solution.py:121
  964.1 1.6 copy-start.3
  971.1 233.5 %reduce-scatter.9.cloned.1.call-start = ((), (), s32[]{:S(2)}) async-start(), calls=%async_computation.9 | async-start | bytes 10027008 | tf_op jit(solution)/shard_map/reduce_scatter | solution.py:122
  978.4 935.1 %reduce-scatter.13.cloned.1.call-start = ((), (), s32[]{:S(2)}) async-start(), calls=%async_computation.11 | async-start | bytes 164192256
  978.4 6.1 copy-start.2
  984.5 5.3 copy-start.14
  984.5 5.3 copy-start.15
  989.8 1.9 copy-start.13
Sparse Core Ops, SparseCore 0:
  10.2 277.7 all-gather.4
  290.3 36.6 all-gather.6
  329.2 36.6 all-gather.8
  368.0 36.6 all-gather.10
  954.9 79.4 reduce-scatter.10
  1039.5 80.2 reduce-scatter.6
  1125.1 79.4 reduce-scatter.8
  1210.2 703.2 reduce-scatter.12
where the time goes:
time: 1930 us; the launch traced here: 1920 us
  waiting for transfers between devices  1200 us (62%)
  matrix products  455 us (24%)
  other arithmetic  145 us (8%)
  local copies, waits for them, and re-layouts  51.4 us (3%)
  blocking collectives  32.6 us (2%)
  loops' own time  20.6 us (1%)
    unnamed x9, waiting for transfers between devices  712 us
    all_gather x1, waiting for transfers between devices, local_step(): embed_full = lax.all_gather(emb_shard, 'fsdp', tiled=True)  278 us
    dot_general x35, matrix products, dot_last(): lax.dot_general(left_mat, right_mat, (((1,), (1,)), ((), ())), preferred_...  224 us
    dot_general x19, matrix products, dot_plain(): lax.dot_general(left_mat, right_mat, (((1,), (0,)), ((), ())), preferred_...  126 us
    dot_general x19, matrix products, dot_first(): lax.dot_general(left_mat, right_mat, (((0,), (0,)), ((), ())), preferred_...  105 us
    reduce_scatter x1, waiting for transfers between devices, local_step(): d_up = lax.psum_scatter(d_up, 'fsdp', scatter_dimension=0, tiled=True)  84.7 us
    reduce_sum x16, other arithmetic, chunk_step(): lab_logit = lab_logit + jnp.sum(jnp.where(label_hit, logits, 0.0), axis=1)  73.7 us
    scatter-add x1, other arithmetic, local_step(): d_full = d_head.at[ids_flat].add(d_x.astype(jnp.float32) * emb_scale)  67.1 us
  transfers between devices with their start and end apart: 8, of which 7 were waited for; matrix products, arithmetic and copies ran while one was open for 6% of the time, Pallas kernels for 0%

commit v1 on v0

v1 whole, which is shorter than its diff:
```python
import math
import jax
import jax.numpy as jnp
from jax import lax
from jax.experimental import pallas as pl
from jax.experimental.pallas import tpu as pltpu
from jax.sharding import PartitionSpec as P

NORM_EPS = 1e-6
LOG2E = 1.4426950408889634
MESH = pl.DeviceIdType.MESH
ANY = pl.BlockSpec(memory_space=pl.ANY)
VMEM = pl.BlockSpec(memory_space=pltpu.VMEM)
BF = jnp.bfloat16
F32 = jnp.float32

SHARD = 3144
HALF = 3200
VP = 2 * HALF
D = 768
FF = 3072
TOK = 512
UNIT = 256
NB = 8
TB = 512
GT = NB * TOK
VT = 1280
NT = VP // VT
NQ = NB * NT
CAP = 128
TOTAL = 8192

BLOCKS = [[(0, 0), (0, 1)], [(2, 1), (1, 1)], [(4, 1), (1, 0)], [(4, 0), (2, 0)],
          [(3, 1), (6, 1)], [(5, 1), (3, 0)], [(6, 0), (5, 0)], [(7, 0), (7, 1)]]
UNITS = [u for b in BLOCKS for u in b]
POS = {u: i for i, u in enumerate(UNITS)}


def dot_plain(a, b):
    return lax.dot_general(a, b, (((1,), (0,)), ((), ())), preferred_element_type=F32)


def dot_last(a, b):
    return lax.dot_general(a, b, (((1,), (1,)), ((), ())), preferred_element_type=F32)


def dot_first(a, b):
    return lax.dot_general(a, b, (((0,), (0,)), ((), ())), preferred_element_type=F32)


def peer_of(me, r):
    p = me
    if r & 1:
        p = p + 2 - 4 * ((me // 2) % 2)
    if r & 2:
        p = p + 4 - 8 * ((me // 4) % 2)
    if r & 4:
        p = p + 8 - 16 * (me // 8)
    return p


def barrier_with(peers):
    sem = pltpu.get_barrier_semaphore()
    for p in peers:
        pl.semaphore_signal(sem, inc=1, device_id=(p,), device_id_type=MESH)
    pl.semaphore_wait(sem, len(peers))


def remote(src, dst, ssem, rsem, dev):
    return pltpu.make_async_remote_copy(src_ref=src, dst_ref=dst, send_sem=ssem, recv_sem=rsem,
                                        device_id=(dev,), device_id_type=MESH)


def params(cid, mib=60):
    return pltpu.CompilerParams(collective_id=cid, has_side_effects=True, vmem_limit_bytes=mib * 2 ** 20)


def pair_kernel(e_ref, out_ref, buf, zero, sems, ssem, rsem):
    me = lax.axis_index('fsdp')
    other = me + 1 - 2 * (me % 2)
    barrier_with([other])
    load = pltpu.make_async_copy(e_ref, buf, sems.at[0])
    load.start()
    zero[...] = jnp.zeros_like(zero)
    load.wait()
    send = remote(buf, out_ref.at[pl.ds(HALF, SHARD)], ssem, rsem, other)
    send.start()
    copies = [pltpu.make_async_copy(buf, out_ref.at[pl.ds(0, SHARD)], sems.at[1]),
              pltpu.make_async_copy(zero, out_ref.at[pl.ds(SHARD, HALF - SHARD)], sems.at[2]),
              pltpu.make_async_copy(zero, out_ref.at[pl.ds(HALF + SHARD, HALF - SHARD)], sems.at[3])]
    for c in copies:
        c.start()
    for c in copies:
        c.wait()
    send.wait()


def pair_gather(e_shard):
    return pl.pallas_call(
        pair_kernel, in_specs=[ANY], out_specs=ANY, out_shape=jax.ShapeDtypeStruct((VP, D), BF),
        scratch_shapes=[pltpu.VMEM((SHARD, D), BF), pltpu.VMEM((HALF - SHARD, D), BF), pltpu.SemaphoreType.DMA((4,)),
                        pltpu.SemaphoreType.DMA, pltpu.SemaphoreType.DMA],
        compiler_params=params(0, 16), name='pair_gather')(e_shard)


def swap_kernel(in_ref, out_ref, recv, ssem, rsem):
    me = lax.axis_index('fsdp')
    peers = [peer_of(me, r) for r in range(1, NB)]
    barrier_with(peers)
    sends = [remote(in_ref.at[r], recv.at[r], ssem.at[r], rsem.at[r], peers[r - 1]) for r in range(1, NB)]
    for s in sends:
        s.start()
    out_ref[0] = in_ref[0]
    for r in range(1, NB):
        sends[r - 1].wait()
        out_ref[r] = recv[r]


def swap(rows, cid):
    return pl.pallas_call(
        swap_kernel, in_specs=[VMEM], out_specs=VMEM, out_shape=jax.ShapeDtypeStruct((NB, CAP, D), BF),
        scratch_shapes=[pltpu.VMEM((NB, CAP, D), BF), pltpu.SemaphoreType.DMA((NB,)), pltpu.SemaphoreType.DMA((NB,))],
        compiler_params=params(cid, 16), name='swap')(rows)


def mask_pads(s, j):
    @pl.when(j == 2)
    def _():
        s[pl.ds(SHARD - 2 * VT, HALF - SHARD), :] = jnp.full((HALF - SHARD, TB), -jnp.inf, F32)

    @pl.when(j == 4)
    def _():
        s[pl.ds(HALF + SHARD - 4 * VT, HALF - SHARD), :] = jnp.full((HALF - SHARD, TB), -jnp.inf, F32)


AG_PATHS = ([(0, a, 0, D) for a in range(3)] + [(2, 0, 0, D), (4, 1, 0, D), (1, 2, 0, D)]
            + [(6, 0, 0, 256), (5, 1, 256, 512), (3, 2, 512, D)])
AG_LIST = [(s, h, a, lo, hi) for h in (1, 0) for (s, a, lo, hi) in AG_PATHS]


def fwd_kernel(hn_ref, e_ref, all_ref, lse_ref, e_v, hn_s, s0, s1, st, stat, csem, ssem, rsem, ssem2, rsem2):
    me = lax.axis_index('fsdp')
    nbr = [peer_of(me, 1 << a) for a in range(3)]
    peers = [peer_of(me, r) for r in range(1, NB)]
    barrier_with(peers)
    load_e = pltpu.make_async_copy(e_ref, e_v, csem.at[0])
    load_e.start()
    load_h = pltpu.make_async_copy(hn_ref, hn_s.at[pl.ds(0, TOK)], csem.at[1])
    load_h.start()
    load_h.wait()

    def piece(k):
        s, h, a, lo, hi = AG_LIST[k]
        src = hn_s.at[pl.ds(POS[(s, h)] * UNIT, UNIT), pl.ds(lo, hi - lo)]
        dst = hn_s.at[pl.ds(POS[(s ^ (1 << a), h)] * UNIT, UNIT), pl.ds(lo, hi - lo)]
        return remote(src, dst, ssem.at[k], rsem.at[k], nbr[a])

    def forward(unit):
        for k, (s, h, a, lo, hi) in enumerate(AG_LIST):
            if (s, h) == unit:
                piece(k).start()

    def arrive(units):
        for unit in units:
            for k, (s, h, a, lo, hi) in enumerate(AG_LIST):
                if (s ^ (1 << a), h) == unit:
                    piece(k).wait_recv()
            forward(unit)

    forward((0, 1))
    forward((0, 0))
    st[:, 0] = jnp.full((NB, 8, TB), -jnp.inf, F32)
    st[:, 1] = jnp.zeros((NB, 8, TB), F32)
    load_e.wait()

    def sdot(q):
        off = pl.multiple_of(lax.rem(q, NT) * VT, VT)
        tok = pl.multiple_of(lax.div(q, NT) * TB, TB)
        return dot_last(e_v[pl.ds(off, VT), :], hn_s[pl.ds(tok, TB), :])

    def proc(q, s):
        mask_pads(s, lax.rem(q, NT))
        blk = lax.div(q, NT)
        s3 = s[...].reshape(VT // 8, 8, TB)
        m8 = st[blk, 0]
        nm = jnp.maximum(m8, s3.max(0))
        st[blk, 1] = st[blk, 1] * jnp.exp2((m8 - nm) * LOG2E) + jnp.exp2((s3 - nm[None]) * LOG2E).sum(0)
        st[blk, 0] = nm

    s0[...] = sdot(0)

    def body(i, carry):
        q = 2 * i
        for block, units in ((1, [(2, 1), (1, 1), (4, 1)]), (2, [(1, 0), (4, 0), (2, 0)]),
                             (4, [(3, 1), (6, 1), (5, 1)]), (5, [(3, 0), (6, 0), (5, 0)]), (7, [(7, 0), (7, 1)])):
            @pl.when(i == (block * NT - 1) // 2)
            def _(units=units):
                arrive(units)
        s1[...] = sdot(q + 1)
        proc(q, s0)
        s0[...] = sdot(jnp.minimum(q + 2, NQ - 1))
        proc(q + 1, s1)
        return carry

    lax.fori_loop(0, NQ // 2, body, 0)
    out = pltpu.make_async_copy(hn_s, all_ref, csem.at[2])
    out.start()

    def unit_stat(unit):
        blk, at = POS[unit] // 2, (POS[unit] % 2) * UNIT
        m8, s8 = st[blk, 0, :, at:at + UNIT], st[blk, 1, :, at:at + UNIT]
        m = m8.max(0, keepdims=True)
        return m, (s8 * jnp.exp2((m8 - m) * LOG2E)).sum(0, keepdims=True)

    for r in range(NB):
        for h in range(2):
            m, s = unit_stat((r, h))
            stat[0, 2 * r:2 * r + 1, h * UNIT:(h + 1) * UNIT] = m
            stat[0, 2 * r + 1:2 * r + 2, h * UNIT:(h + 1) * UNIT] = s
    sends = [remote(stat.at[0], stat.at[r], ssem2.at[r], rsem2.at[r], peers[r - 1]) for r in range(1, NB)]
    for c in sends:
        c.start()
    for c in sends:
        c.wait()
    for r in range(NB):
        ms = [stat[k, 2 * (k ^ r):2 * (k ^ r) + 1, :] for k in range(NB)]
        ss = [stat[k, 2 * (k ^ r) + 1:2 * (k ^ r) + 2, :] for k in range(NB)]
        top = ms[0]
        for m in ms[1:]:
            top = jnp.maximum(top, m)
        tot = jnp.zeros_like(top)
        for m, s in zip(ms, ss):
            tot = tot + s * jnp.exp2((m - top) * LOG2E)
        lse = top + jnp.log(tot)
        for h in range(2):
            blk, at = POS[(r, h)] // 2, (POS[(r, h)] % 2) * UNIT
            lse_ref[blk, :, at:at + UNIT] = lse[:, h * UNIT:(h + 1) * UNIT]
    for k in range(len(AG_LIST)):
        piece(k).wait_send()
    out.wait()


def head_forward(hn, e_loc):
    n = len(AG_LIST)
    return pl.pallas_call(
        fwd_kernel, in_specs=[ANY, ANY], out_specs=[ANY, VMEM],
        out_shape=[jax.ShapeDtypeStruct((GT, D), BF), jax.ShapeDtypeStruct((NB, 1, TB), F32)],
        scratch_shapes=[pltpu.VMEM((VP, D), BF), pltpu.VMEM((GT, D), BF), pltpu.VMEM((VT, TB), F32), pltpu.VMEM((VT, TB), F32),
                        pltpu.VMEM((NB, 2, 8, TB), F32), pltpu.VMEM((NB, 16, TB), F32), pltpu.SemaphoreType.DMA((3,)),
                        pltpu.SemaphoreType.DMA((n,)), pltpu.SemaphoreType.DMA((n,)),
                        pltpu.SemaphoreType.DMA((NB,)), pltpu.SemaphoreType.DMA((NB,))],
        compiler_params=params(1), name='head_fwd')(hn, e_loc)


RS_PATHS = [(7, 0, 0, 256), (7, 1, 256, 512), (7, 2, 512, D),
            (5, 2, 0, 384), (5, 0, 384, D), (6, 1, 0, 384), (6, 2, 384, D), (3, 0, 0, 384), (3, 1, 384, D),
            (1, 0, 0, D), (2, 1, 0, D), (4, 2, 0, D)]
RS_LIST = [(s, h, a, lo, hi) for (s, a, lo, hi) in RS_PATHS for h in range(2)]


def rs_place(k):
    s, h, a, lo, hi = RS_LIST[k]
    t = s ^ (1 << a)
    if s == 7:
        return 0, {6: 0, 5: 1, 3: 2}[t] * 2 + h, 0
    if t:
        return 1, {1: 0, 2: 1, 4: 2}[t] * 2 + h, lo
    return 2, a * 2 + h, 0


def bwd_kernel(hn_ref, e_ref, lse_ref, lab_ref, dh_ref, g_ref, l_ref,
               e_v, hn_s, s0, s1, g0, g1, dh, ra, rb, rc, csem, gsem, ssem, rsem):
    me = lax.axis_index('fsdp')
    nbr = [peer_of(me, 1 << a) for a in range(3)]
    barrier_with(nbr)
    load_e = pltpu.make_async_copy(e_ref, e_v, csem.at[0])
    load_e.start()
    load_h = pltpu.make_async_copy(hn_ref, hn_s, csem.at[1])
    load_h.start()
    dh[...] = jnp.zeros_like(dh)
    l_ref[...] = jnp.zeros_like(l_ref)
    bufs = (ra, rb, rc)

    def piece(k):
        s, h, a, lo, hi = RS_LIST[k]
        src = dh.at[pl.ds(POS[(s, h)] * UNIT, UNIT), pl.ds(lo, hi - lo)]
        b, i, c = rs_place(k)
        return remote(src, bufs[b].at[i, :, pl.ds(c, hi - lo)], ssem.at[k], rsem.at[k], nbr[a])

    def finish(block):
        for unit in BLOCKS[block]:
            rows = pl.ds(POS[unit] * UNIT, UNIT)
            for k, (s, h, a, lo, hi) in enumerate(RS_LIST):
                if (s ^ (1 << a), h) == unit:
                    piece(k).wait_recv()
                    b, i, c = rs_place(k)
                    dh[rows, lo:hi] += bufs[b][i, :, c:c + hi - lo]
            for k, (s, h, a, lo, hi) in enumerate(RS_LIST):
                if (s, h) == unit:
                    piece(k).start()

    def place(q):
        return NB - 1 - lax.div(q, NT), pl.multiple_of(lax.rem(q, NT) * VT, VT)

    def sdot(q):
        blk, off = place(q)
        return dot_last(e_v[pl.ds(off, VT), :], hn_s[pl.ds(pl.multiple_of(blk * TB, TB), TB), :])

    iota = lax.broadcasted_iota(jnp.int32, (VT, TB), 0)

    def g_copy(q, g, k):
        blk, off = place(q)
        return pltpu.make_async_copy(g, g_ref.at[pl.ds(off, VT), pl.ds(pl.multiple_of(blk * TB, TB), TB)], gsem.at[k])

    def proc(q, s, g, k):
        blk, off = place(q)
        mask_pads(s, lax.rem(q, NT))

        @pl.when(q >= 2)
        def _():
            g_copy(q, g, k).wait()
        w = s[...] - lse_ref[blk]
        hit = iota == (lab_ref[blk] - off)
        p = jnp.exp2(w * LOG2E - 13.0)
        gv = (p - jnp.where(hit, 2.0 ** -13, 0.0)).astype(BF)
        l_ref[...] += jnp.where(hit, w, 0.0).reshape(VT // 8, 8, TB).sum(0)
        g[...] = gv
        rows = pl.ds(pl.multiple_of(blk * TB, TB), TB)
        dh[rows, :] += dot_first(gv, e_v[pl.ds(off, VT), :])

    def after(q, g, k):
        g_copy(q, g, k).start()
        for i in range(NB):
            @pl.when(q == i * NT + NT - 1)
            def _(i=i):
                finish(NB - 1 - i)

    load_e.wait()
    load_h.wait()
    s0[...] = sdot(0)

    def body(i, carry):
        q = 2 * i
        s1[...] = sdot(q + 1)
        proc(q, s0, g0, 0)
        after(q, g0, 0)
        s0[...] = sdot(jnp.minimum(q + 2, NQ - 1))
        proc(q + 1, s1, g1, 1)
        after(q + 1, g1, 1)
        return carry

    lax.fori_loop(0, NQ // 2, body, 0)
    g_copy(NQ - 2, g0, 0).wait()
    g_copy(NQ - 1, g1, 1).wait()
    dh_ref[...] = dh[pl.ds(0, TOK), :]
    for k in range(len(RS_LIST)):
        piece(k).wait_send()


def head_backward(hn_all, e_loc, lse, lab):
    n = len(RS_LIST)
    return pl.pallas_call(
        bwd_kernel, in_specs=[ANY, ANY, VMEM, VMEM], out_specs=[VMEM, ANY, VMEM],
        out_shape=[jax.ShapeDtypeStruct((TOK, D), F32), jax.ShapeDtypeStruct((VP, GT), BF), jax.ShapeDtypeStruct((8, TB), F32)],
        scratch_shapes=[pltpu.VMEM((VP, D), BF), pltpu.VMEM((GT, D), BF), pltpu.VMEM((VT, TB), F32), pltpu.VMEM((VT, TB), F32),
                        pltpu.VMEM((VT, TB), BF), pltpu.VMEM((VT, TB), BF), pltpu.VMEM((GT, D), F32),
                        pltpu.VMEM((6, UNIT, 256), F32), pltpu.VMEM((6, UNIT, D), F32), pltpu.VMEM((6, UNIT, D), F32),
                        pltpu.SemaphoreType.DMA((2,)), pltpu.SemaphoreType.DMA((2,)),
                        pltpu.SemaphoreType.DMA((n,)), pltpu.SemaphoreType.DMA((n,))],
        compiler_params=params(2), name='head_bwd')(hn_all, e_loc, lse, lab)


DE_T = 640


def de_kernel(scale, g_ref, hn_ref, rows_ref, dx_ref, out_ref):
    out_ref[...] = dot_plain(g_ref[...], hn_ref[...])
    base = pl.program_id(0) * DE_T
    iota = lax.broadcasted_iota(jnp.int32, (DE_T, NB * CAP), 0)
    pick = jnp.where(iota == rows_ref[...] - base, 1.0, 0.0).astype(BF)
    out_ref[...] += dot_plain(pick, dx_ref[...]) * scale


def embed_grad(g, hn_all, rows, dx, scale):
    import functools
    n = NB * CAP
    return pl.pallas_call(
        functools.partial(de_kernel, scale), grid=(VP // DE_T,),
        in_specs=[pl.BlockSpec((DE_T, GT), lambda j: (j, 0)), pl.BlockSpec((GT, D), lambda j: (0, 0)),
                  pl.BlockSpec((1, n), lambda j: (0, 0)), pl.BlockSpec((n, D), lambda j: (0, 0))],
        out_specs=pl.BlockSpec((DE_T, D), lambda j: (j, 0)), out_shape=jax.ShapeDtypeStruct((VP, D), F32),
        compiler_params=pltpu.CompilerParams(vmem_limit_bytes=60 * 2 ** 20),
        cost_estimate=pl.CostEstimate(flops=2 * VP * (GT + n) * D, bytes_accessed=VP * GT * 2 + VP * D * 4, transcendentals=0),
        name='embed_grad')(g, hn_all, rows, dx)


def rms_apply(values, gain_vec):
    inv_rms = lax.rsqrt(jnp.mean(values * values, axis=-1, keepdims=True) + NORM_EPS)
    return (values * inv_rms * gain_vec).astype(BF), inv_rms


def rms_backward(values, inv_rms, gain_vec, grad_out):
    scaled = grad_out * gain_vec
    return inv_rms * scaled - values * (inv_rms ** 3) * jnp.mean(scaled * values, axis=-1, keepdims=True)


def solution(mesh):
    def local_step(ids_blk, lab_blk, emb_shard, gate_shard, up_shard, down_shard, gain_mlp, gain_final):
        me = lax.axis_index('fsdp')
        core, chip = me % 2, me // 2
        scale = math.sqrt(D)
        both = lax.all_gather(jnp.concatenate([ids_blk, lab_blk]), 'fsdp')
        w_gu = lax.all_gather(jnp.concatenate([gate_shard, up_shard], 1), 'fsdp', tiled=True)
        w_down = lax.all_gather(down_shard, 'fsdp', tiled=True)
        e_loc = pair_gather(emb_shard)

        rel = jnp.stack([peer_of(me, r) for r in range(NB)])
        grp = jnp.take(both, rel, axis=0)
        ids, labs = grp[:, 0], grp[:, 1]

        def local_row(v):
            within = v % (2 * SHARD)
            row = jnp.where(within // SHARD == core, 0, HALF) + within % SHARD
            return jnp.where(v // (2 * SHARD) == chip, row, -1)

        rows = local_row(ids)
        lab_row = local_row(labs)
        mine = (rows >= 0).astype(F32)
        before = (jnp.arange(TOK)[:, None] < jnp.arange(TOK)[None, :]).astype(F32)
        rank = dot_plain(mine, before).astype(jnp.int32)
        slots = jnp.arange(CAP, dtype=jnp.int32)
        own_chip = ids[0] // (2 * SHARD)
        own_rel = jnp.bitwise_xor(own_chip, chip)
        is_rel = own_rel[None, :] == jnp.arange(NB)[:, None]
        own_rank_all = dot_plain(is_rel.astype(F32), before)
        own_rank = jnp.sum(jnp.where(is_rel, own_rank_all, 0.0), 0).astype(jnp.int32)
        counts = jnp.sum((both[:, 0] // (2 * SHARD))[:, None, :] == jnp.arange(NB)[None, :, None], axis=-1)
        rounds = (jnp.max(counts) + CAP - 1) // CAP

        def slot_rows(rnd):
            want = (rows[:, None, :] >= 0) & (rank[:, None, :] - rnd * CAP == slots[None, :, None])
            got = jnp.sum(jnp.where(want, rows[:, None, :] + 1, 0), axis=-1) - 1
            return got.reshape(NB * CAP)

        def slot_tokens(rnd):
            want = is_rel[:, None, :] & (own_rank[None, None, :] - rnd * CAP == slots[None, :, None])
            return jnp.sum(jnp.where(want, jnp.arange(TOK)[None, None, :], 0), axis=-1).reshape(NB * CAP)

        def lookup(rnd, x, cid):
            out = jnp.take(e_loc, jnp.maximum(slot_rows(rnd), 0), axis=0, mode='clip').reshape(NB, CAP, D)
            got = swap(out, cid).reshape(NB * CAP, D)
            here = own_rank // CAP == rnd
            at = jnp.where(here, own_rel * CAP + own_rank % CAP, 0)
            return jnp.where(here[:, None], jnp.take(got, at, axis=0, mode='clip'), x)

        x_bf = lookup(0, jnp.zeros((TOK, D), BF), 3)
        x_bf = lax.while_loop(lambda c: c[0] < rounds, lambda c: (c[0] + 1, lookup(c[0], c[1], 4)), (jnp.int32(1), x_bf))[1]

        x_emb = x_bf.astype(F32) * scale
        normed, inv_first = rms_apply(x_emb, gain_mlp)
        gu = dot_plain(normed, w_gu).astype(BF)
        gate, up_val = gu[:, :FF].astype(F32), gu[:, FF:].astype(F32)
        hidden_act = (jax.nn.silu(gate) * up_val).astype(BF)
        mlp_out = dot_plain(hidden_act, w_down).astype(BF)
        hid32 = (x_emb + mlp_out.astype(F32)).astype(BF).astype(F32)
        hid_norm, inv_final = rms_apply(hid32, gain_final)

        hn_all, lse = head_forward(hid_norm, e_loc)
        lab_pos = jnp.concatenate([lab_row[r, h * UNIT:(h + 1) * UNIT] for r, h in UNITS]).reshape(NB, 1, TB)
        d_hid, g_all, loss8 = head_backward(hn_all, e_loc, lse, lab_pos)
        loss = lax.psum(-jnp.sum(loss8), 'fsdp') * (1.0 / TOTAL)

        d_hidden = rms_backward(hid32, inv_final, gain_final, d_hid)
        d_mlp = d_hidden.astype(BF)
        d_down = lax.psum_scatter(dot_first(hidden_act, d_mlp), 'fsdp', scatter_dimension=0, tiled=True)
        d_act = dot_last(d_mlp, w_down)
        sig = jax.nn.sigmoid(gate)
        d_gate_pre = (d_act * up_val * sig * (1.0 + gate * (1.0 - sig))).astype(BF)
        d_up_pre = (d_act * gate * sig).astype(BF)
        d_gu_pre = jnp.concatenate([d_gate_pre, d_up_pre], 1)
        d_gu = lax.psum_scatter(dot_first(normed, d_gu_pre), 'fsdp', scatter_dimension=0, tiled=True)
        d_normed = dot_last(d_gu_pre, w_gu)
        d_x = (d_hidden + rms_backward(x_emb, inv_first, gain_mlp, d_normed)).astype(BF)

        def send_dx(rnd, cid):
            return swap(jnp.take(d_x, slot_tokens(rnd), axis=0, mode='clip').reshape(NB, CAP, D), cid).reshape(NB * CAP, D)

        d_loc = embed_grad(g_all, hn_all, slot_rows(0)[None, :], send_dx(0, 5), scale)

        def more(c):
            rnd, acc = c
            at = slot_rows(rnd)
            add = jnp.where((at >= 0)[:, None], send_dx(rnd, 6).astype(F32) * scale, 0.0)
            return rnd + 1, acc.at[jnp.maximum(at, 0)].add(add)

        d_loc = lax.while_loop(lambda c: c[0] < rounds, more, (jnp.int32(1), d_loc))[1]
        pairs = [(d, d ^ 1) for d in range(2 * NB)]
        d_embed = d_loc[:SHARD] + lax.ppermute(d_loc[HALF:HALF + SHARD], 'fsdp', pairs)
        return loss, d_embed, d_gu[:, :FF], d_gu[:, FF:], d_down

    shard = P('fsdp', None)
    return jax.shard_map(local_step, mesh=mesh, in_specs=(shard,) * 6 + (P(), P()),
                         out_specs=(P(), shard, shard, shard, shard), check_vma=False)
```

time: 1930 us -> 601 us (0.31)
  waiting for transfers between devices: 1200 us -> 43.7 us
  matrix products: 455 us -> 57.1 us
  Pallas kernels: 0 us -> 360 us
  other arithmetic: 145 us -> 23.5 us
  blocking collectives: 32.6 us -> 57.7 us
  loops' own time: 20.6 us -> 0.37 us
    unnamed x9 -> x4, waiting for transfers between devices: 712 us -> 0.74 us
    dot_general x73 -> x8, matrix products: 455 us -> 57.1 us  [the longest x2 19.5 us: dot_first(): lax.dot_general(a, b, (((0,), (0,)), ((), ())), preferred_element_type=F32)]
    pallas_call x0 -> x6, Pallas kernels: none -> 360 us  [the longest x1 149 us: head_backward(): pl.pallas_call(bwd_kernel, in_specs=[ANY, ANY, VMEM, VMEM], out_specs=[VM...]
    all_gather x3 -> x1, waiting for transfers between devices: 344 us -> 0.02 us  [local_step(): lax.all_gather(jnp.concatenate([gate_shard, up_shard], 1), 'fsdp', tiled=...]
    reduce_scatter x3 -> x2, waiting for transfers between devices: 112 us -> 24.9 us  [the longest x1 24.9 us: local_step(): lax.psum_scatter(dot_first(hidden_act, d_mlp), 'fsdp', scatter_dimension=...]
    reduce_sum x17 -> x4, other arithmetic: 74.3 us -> 1.88 us  [the longest x1 0.6 us: local_step(): loss = lax.psum(-jnp.sum(loss8), 'fsdp') * (1.0 / TOTAL)]
    scatter-add x1 -> x0, other arithmetic: 67.1 us -> none  [local_step(): d_full = d_head.at[ids_flat].add(d_x.astype(jnp.float32) * emb_scale)]
    while x48 -> x0, local copies, waits for them, and re-layouts: 27 us -> none
  transfers between devices with their start and end apart: 8 -> 5, of which waited for: 7 -> 2; matrix products, arithmetic and copies ran while one was open for 6% -> 13% of each run, Pallas kernels for 0% -> 21%
where the time goes in v1:
time: 601 us; the launch traced here: 593 us
  Pallas kernels  360 us (60%)
  blocking collectives  57.7 us (10%)
  matrix products  57.1 us (10%)
  waiting for transfers between devices  43.7 us (7%)
  local copies, waits for them, and re-layouts  33.2 us (6%)
  other arithmetic  23.5 us (4%)
  between operations  17.8 us (3%)
    pallas_call x1, Pallas kernels, head_backward(): pl.pallas_call(bwd_kernel, in_specs=[ANY, ANY, VMEM, VMEM], out_specs=[VM...  149 us
    pallas_call x1, Pallas kernels, head_forward(): pl.pallas_call(fwd_kernel, in_specs=[ANY, ANY], out_specs=[ANY, VMEM], ou...  88.8 us
    pallas_call x1, Pallas kernels, embed_grad(): pl.pallas_call(functools.partial(de_kernel, scale), grid=(VP // DE_T,), i...  58.7 us
    pallas_call x2, Pallas kernels, swap(): pl.pallas_call(swap_kernel, in_specs=[VMEM], out_specs=VMEM, out_shape=ja...  54.3 us
    psum x1, blocking collectives, local_step(): loss = lax.psum(-jnp.sum(loss8), 'fsdp') * (1.0 / TOTAL)  42.6 us
    reduce_scatter x1, waiting for transfers between devices, local_step(): lax.psum_scatter(dot_first(hidden_act, d_mlp), 'fsdp', scatter_dimension=...  24.9 us
    dot_general x2, matrix products, dot_first(): lax.dot_general(a, b, (((0,), (0,)), ((), ())), preferred_element_type=F32)  19.5 us
    dot_general x4, matrix products, dot_plain(): lax.dot_general(a, b, (((1,), (0,)), ((), ())), preferred_element_type=F32)  19.4 us
  transfers between devices with their start and end apart: 5, of which 2 were waited for; matrix products, arithmetic and copies ran while one was open for 13% of the time, Pallas kernels for 21%

profile of v1, /device:TPU:0, one launch (start us, length us, event | category | flops | bytes accessed | tf_op | source)
XLA Modules:
  0.0 593.0 jit_solution(3965034809205349978)
XLA Ops:
  7.2 1.9 pad_maximum_fusion.5
  9.2 0.7 all-gather.7.cloned.1.call-update
  10.1 15.0 %all-gather.1 = s32[16,2,512]{2,1,0:T(2,128)S(1)} all-gather(s32[1,2,512]{2,1,0:T(2,128)S(1)} %add_bitcast_fusion.1), channel_id=2, replica_groups=mesh['fsdp'=16] {'fsdp'}, dimensions={0}, use_global_device_ids=true | all-gather | bytes 69632 | tf_op jit(solution)/shard_map/all_gather | solution.py:412
  25.1 0.2 and_select_fusion.2
  25.3 0.4 convert_reduce_fusion
  25.6 0.6 reduce_max.9
  27.0 0.1 stack.53
  27.1 0.1 stack.62
  27.2 0.6 gather_fusion.3
  27.8 0.1 broadcast_select_fusion.2
  27.9 0.2 fusion.43
  28.5 0.2 convolution_convert_fusion.2
  28.7 0.5 select_reduce_fusion.4
  29.2 2.4 copy-done
  31.6 8.6 %pair_gather.1.e_ref = bf16[6400,768]{1,0:T(8,128)(2,1)} custom-call(bf16[3144,768]{1,0:T(8,128)(2,1)S(1)} %copy-done), custom_call_target="tpu_custom_call" | custom-call | tf_op jit(solution)/shard_map/pair_gather/pallas_call | solution.py:99
  40.1 9.5 %gather_fusion.4 = bf16[1024,768]{1,0:T(8,128)(2,1)S(1)} fusion(bf16[6400,768]{1,0:T(8,128)(2,1)} %pair_gather.1.e_ref, s32[1024]{0:T(1024)S(1)} %bitcast_clamp_fusion.3), kind=kCustom, calls=%fused_computation.4 | custom fusion | bytes 3149824 | tf_op jit(solution)/shard_map/jit(_take)/gather | solution.py:450
  49.7 33.3 %swap.12 = bf16[8,128,768]{2,1,0:T(8,128)(2,1)S(1)} custom-call(bf16[8,128,768]{2,1,0:T(8,128)(2,1)S(1)} %bitcast.159), custom_call_target="tpu_custom_call" | custom-call | tf_op jit(solution)/shard_map/swap/pallas_call | solution.py:120
  83.2 2.0 gather_fusion.5
  85.2 1.0 broadcast_select_fusion.1
  86.2 0.2 while.29
  86.4 1.4 fusion.27
  87.9 11.0 %convolution_convert_fusion = bf16[512,6144]{1,0:T(8,128)(2,1)} fusion(bf16[768,6144]{1,0:T(8,128)(2,1)} %all-gather.5.cloned.1.call-done, bf16[512,768]{1,0:T(8,128)(2,1)} %get-tuple-element.349, f32[768]{0:T(1024)S(1)} %copy-done.14, f32[512]{0:T(512)S(1)} %get-tuple-element.491), kind=kOutput, calls=%fused_computation.54 | convolution fusion | flops 4836556800 | bytes 16520192 | tf_op jit(solution)/shard_map/dot_general | solution.py:40
  98.9 18.1 %all-gather.7.cloned.1.call-done = bf16[3072,768]{1,0:T(8,128)(2,1)} async-done(((bf16[192,768]{1,0:T(8,128)(2,1)}), bf16[3072,768]{1,0:T(8,128)(2,1)}) %all-gather.7.cloned.1.call-update) | async-done | bytes 4718608 | tf_op jit(solution)/shard_map/all_gather | solution.py:414
  117.0 8.0 %fusion.36 = (f32[512]{0:T(512)S(1)}, bf16[512,768]{1,0:T(8,128)(2,1)S(1)}) fusion(bf16[3072,768]{1,0:T(8,128)(2,1)} %all-gather.7.cloned.1.call-done, bf16[512,6144]{1,0:T(8,128)(2,1)} %convolution_convert_fusion, bf16[512,768]{1,0:T(8,128)(2,1)S(1)} %copy-done.4), kind=kOutput, calls=%fused_computation.93 | convolution fusion | flops 2432040448 | bytes 12584960 | tf_op jit(solution)/shard_map/dot_general | solution.py:40
  125.0 1.1 fusion.38.hn_ref
  126.1 88.8 %head_fwd.1 = (bf16[4096,768]{1,0:T(8,128)(2,1)}, f32[8,1,512]{2,1,0:T(1,128)}) custom-call(bf16[512,768]{1,0:T(8,128)(2,1)} %fusion.38.hn_ref, bf16[6400,768]{1,0:T(8,128)(2,1)} %get-tuple-element.696), custom_call_target="tpu_custom_call" | custom-call | tf_op jit(solution)/shard_map/head_fwd/pallas_call | solution.py:245
  214.9 149.3 %head_bwd.1 = (f32[512,768]{1,0:T(8,128)}, bf16[6400,4096]{1,0:T(8,128)(2,1)}, f32[8,512]{1,0:T(8,128)}) custom-call(bf16[4096,768]{1,0:T(8,128)(2,1)} %get-tuple-element.350.hn_ref, bf16[6400,768]{1,0:T(8,128)(2,1)} %get-tuple-element.696, f32[8,1,512]{2,1,0:T(1,128)} %get-tuple-element.351.lse_ref, s32[8,1,512]{2,1,0:T(1,128)} %bitcast.168), custom_call_target="tpu_custom_call" | custom-call | tf_op jit(solution)/shard_map/head_bwd/pallas_call | solution.py:362
  364.2 1.8 fusion.41
  366.1 7.8 %fusion.14 = (bf16[512,3072]{1,0:T(8,128)(2,1)S(1)}, bf16[512,3072]{1,0:T(8,128)(2,1)S(1)}) fusion(bf16[512,6144]{1,0:T(8,128)(2,1)} %convolution_convert_fusion, bf16[3072,768]{1,0:T(8,128)(2,1)} %all-gather.7.cloned.1.call-done, f32[512]{0:T(512)S(1)} %broadcast_multiply_fusion.3, f32[512]{0:T(512)S(1)} %get-tuple-element.493, ...), kind=kOutput, calls=%fused_computation.60 | convolution fusion | flops 2442264576 | bytes 19670016 | tf_op jit(solution)/shard_map/dot_general | solution.py:44
  373.9 1.7 copy-done.10
  375.7 0.9 copy-done.11
  376.5 9.4 %fusion.21 = f32[768,6144]{1,0:T(8,128)} fusion(bf16[512,3072]{1,0:T(8,128)(2,1)S(1)} %get-tuple-element.468, bf16[512,3072]{1,0:T(8,128)(2,1)S(1)} %get-tuple-element.467, bf16[512,768]{1,0:T(8,128)(2,1)S(1)} %copy-done.4, f32[768]{0:T(1024)S(1)} %copy-done.14, f32[512]{0:T(512)S(1)} %get-tuple-element.491), kind=kOutput, calls=%fused_computation.68 | convolution fusion | flops 4845993984 | bytes 25957376 | tf_op jit(solution)/shard_map/dot_general | solution.py:48
  386.1 0.4 select_reduce_fusion.3
  386.5 0.6 broadcast_add_fusion.2
  387.1 10.3 %fusion.29 = (f32[512]{0:T(512)S(1)}, f32[512,768]{1,0:T(8,128)S(1)}) fusion(bf16[512,768]{1,0:T(8,128)(2,1)S(1)} %copy-done.4, f32[768]{0:T(1024)S(1)} %copy-done.14, bf16[768,6144]{1,0:T(8,128)(2,1)} %all-gather.5.cloned.1.call-done, bf16[512,3072]{1,0:T(8,128)(2,1)} %copy-done.11, bf16[512,3072]{1,0:T(8,128)(2,1)} %copy-done.10), kind=kOutput, calls=%fused_computation.86 | convolution fusion | flops 4846386688 | bytes 18093056 | tf_op jit(solution)/shard_map/dot_general | solution.py:44
  397.5 0.9 fusion.35
  398.3 4.0 gather_fusion.6
  402.4 21.1 %swap.13 = bf16[8,128,768]{2,1,0:T(8,128)(2,1)S(1)} custom-call(bf16[8,128,768]{2,1,0:T(8,128)(2,1)S(1)} %bitcast.160), custom_call_target="tpu_custom_call" | custom-call | tf_op jit(solution)/shard_map/swap/pallas_call | solution.py:120
  423.4 1.1 copy-done.1
  424.6 10.1 %fusion.44 = f32[3072,768]{1,0:T(8,128)} fusion(bf16[512,768]{1,0:T(8,128)(2,1)S(1)} %get-tuple-element.499, f32[512,768]{1,0:T(8,128)S(1)} %copy-done.9, f32[512]{0:T(512)S(1)} %broadcast_multiply_fusion.3, f32[512]{0:T(512)S(1)} %get-tuple-element.493, f32[768]{0:T(1024)S(1)} %copy-done.15, f32[512]{0:T(512)S(1)} %get-tuple-element.494, ...), kind=kOutput, calls=%fused_computation.107 | convolution fusion | flops 2431254528 | bytes 18097152 | tf_op jit(solution)/shard_map/dot_general | solution.py:48
  434.7 58.7 %embed_grad.1 = f32[6400,768]{1,0:T(8,128)} custom-call(bf16[6400,4096]{1,0:T(8,128)(2,1)} %get-tuple-element.353.g_ref, bf16[4096,768]{1,0:T(8,128)(2,1)} %get-tuple-element.350.hn_ref, s32[1,1024]{1,0:T(1,128)} %bitcast.187, bf16[1024,768]{1,0:T(8,128)(2,1)} %bitcast.161), custom_call_target="tpu_custom_call" | custom-call | flops 50331648000 | bytes 72089600 | tf_op jit(solution)/shard_map/embed_grad/pallas_call | solution.py:387
  493.4 0.2 while.30
  493.7 8.2 %slice.103 = f32[3144,768]{1,0:T(8,128)} slice(f32[6400,768]{1,0:T(8,128)} %get-tuple-element.355), slice={[3200:6344], [0:768]} | slice | bytes 19316736 | tf_op jit(solution)/shard_map/slice | solution.py:498
  501.9 0.6 reduce_sum.128
  503.1 42.6 %psum.7 = f32[]{:T(128)} all-reduce(f32[]{:T(128)S(6)} %neg.9), channel_id=1, replica_groups=mesh['fsdp'=16] {'fsdp'}, use_global_device_ids=true, to_apply=%region_10.11 | all-reduce | flops 1 | bytes 8 | tf_op jit(solution)/shard_map/psum | solution.py:471
  546.4 11.5 %slice_add_fusion = f32[3144,768]{1,0:T(8,128)} fusion(f32[3144,768]{1,0:T(8,128)} %collective-permute-done, f32[6400,768]{1,0:T(8,128)} %get-tuple-element.355), kind=kLoop, calls=%fused_computation.53 | loop fusion | flops 2414592 | bytes 28975104 | tf_op jit(solution)/shard_map/add | solution.py:498
  558.0 2.3 fusion.88
  560.3 24.9 %reduce-scatter.5.cloned.1.call-done = f32[192,768]{1,0:T(8,128)} async-done(((f32[3072,768]{1,0:T(8,128)}), f32[192,768]{1,0:T(8,128)}) %reduce-scatter.5.cloned.1.call-update) | async-done | bytes 589840 | tf_op jit(solution)/shard_map/reduce_scatter | solution.py:475
  (86 shorter events, 0.9 us)
Async XLA Ops:
  7.2 2.9 copy-start.18
  7.2 2.9 copy-start.19
  7.2 80.7 %all-gather.5.cloned.1.call-start = ((), (), s32[]{:S(2)}) async-start(), calls=%async_computation.2 | async-start | bytes 10027008 | tf_op jit(solution)/shard_map/all_gather | solution.py:413
  9.2 107.8 %all-gather.7.cloned.1.call-start = ((), (), s32[]{:S(2)}) async-start(), calls=%async_computation.3 | async-start | bytes 5013504 | tf_op jit(solution)/shard_map/all_gather | solution.py:414
  9.9 548.0 %reduce-scatter.3.cloned.1.call-start = ((), (), s32[]{:S(2)}) async-start(), calls=%async_computation.4 | async-start | bytes 20054016 | tf_op jit(solution)/shard_map/reduce_scatter | solution.py:481
  29.2 2.4 copy-start
  83.2 2.0 copy-start.17
  86.2 1.6 copy-start.14
  86.4 12.5 %copy-start.5 = (s32[8,512]{1,0:T(8,128)}, s32[8,512]{1,0:T(8,128)S(1)}, u32[]{:S(2)}) copy-start(s32[8,512]{1,0:T(8,128)S(1)} %get-tuple-element.701) | copy-start | bytes 49156
  86.4 12.5 %copy-start.12 = (s32[8,512]{1,0:T(8,128)}, s32[8,512]{1,0:T(8,128)S(1)}, u32[]{:S(2)}) copy-start(s32[8,512]{1,0:T(8,128)S(1)} %get-tuple-element.704) | copy-start | bytes 49156
  87.9 29.1 %copy-start.4 = (bf16[512,768]{1,0:T(8,128)(2,1)S(1)}, bf16[512,768]{1,0:T(8,128)(2,1)}, u32[]{:S(2)}) copy-start(bf16[512,768]{1,0:T(8,128)(2,1)} %get-tuple-element.349) | copy-start | bytes 2359300
  98.9 26.1 %copy-start.15 = (f32[768]{0:T(1024)S(1)}, f32[768]{0:T(1024)}, u32[]{:S(2)}) copy-start(f32[768]{0:T(1024)} %param.19) | copy-start | bytes 9220
  364.2 1.9 copy-start.7
  373.9 1.7 copy-start.10
  373.9 2.6 copy-start.11
  386.0 199.2 %reduce-scatter.5.cloned.1.call-start = ((), (), s32[]{:S(2)}) async-start(), calls=%async_computation.5 | async-start | bytes 10027008 | tf_op jit(solution)/shard_map/reduce_scatter | solution.py:475
  387.1 10.4 %copy-start.8 = (f32[512,768]{1,0:T(8,128)S(1)}, f32[512,768]{1,0:T(8,128)}, u32[]{:S(2)}) copy-start(f32[512,768]{1,0:T(8,128)} %get-tuple-element.354) | copy-start | bytes 4718596
  402.4 22.2 %copy-start.9 = (f32[512,768]{1,0:T(8,128)S(1)}, f32[512,768]{1,0:T(8,128)}, u32[]{:S(2)}) copy-start(f32[512,768]{1,0:T(8,128)} %get-tuple-element.354) | copy-start | bytes 4718596
  423.4 1.1 copy-start.1
  434.7 58.7 %copy-start.6 = (s32[8,512]{1,0:T(8,128)S(1)}, s32[8,512]{1,0:T(8,128)}, u32[]{:S(2)}) copy-start(s32[8,512]{1,0:T(8,128)} %copy-done.5) | copy-start | bytes 49156
  434.7 58.7 %copy-start.13 = (s32[8,512]{1,0:T(8,128)S(1)}, s32[8,512]{1,0:T(8,128)}, u32[]{:S(2)}) copy-start(s32[8,512]{1,0:T(8,128)} %copy-done.12) | copy-start | bytes 49156
  493.7 8.2 %copy-start.16 = (f32[8,512]{1,0:T(8,128)S(1)}, f32[8,512]{1,0:T(8,128)}, u32[]{:S(2)}) copy-start(f32[8,512]{1,0:T(8,128)} %get-tuple-element.352) | copy-start | bytes 49156
  501.9 44.6 %collective-permute-start = (f32[3144,768]{1,0:T(8,128)}, f32[3144,768]{1,0:T(8,128)}, u32[]{:S(2)}, u32[]{:S(2)}) collective-permute-start(f32[3144,768]{1,0:T(8,128)} %slice.103), channel_id=1, source_target_pairs={{0,1},{1,0},{2,3},{3,2},{4,5},{5,4},{6,7},{7,6},{8,9},{9,8},{10,11... | collective-permute-start | bytes 28975112 | tf_op jit(solution)/shard_map/ppermute | solution.py:498
Sparse Core Ops, SparseCore 0:
  10.8 67.2 all-gather.4
  80.3 36.6 all-gather.6
  386.1 113.6 reduce-scatter.2
  504.9 80.2 reduce-scatter.4

commit v2 on v1

--- a/solution.py
+++ b/solution.py
@@ -1,3 +1,4 @@
+import functools
 import math
 import jax
 import jax.numpy as jnp
@@ -29,6 +30,7 @@
 NQ = NB * NT
 CAP = 128
 TOTAL = 8192
+EMB_SCALE = math.sqrt(D)
 
 BLOCKS = [[(0, 0), (0, 1)], [(2, 1), (1, 1)], [(4, 1), (1, 0)], [(4, 0), (2, 0)],
           [(3, 1), (6, 1)], [(5, 1), (3, 0)], [(6, 0), (5, 0)], [(7, 0), (7, 1)]]
@@ -124,13 +126,9 @@
 
 
 def mask_pads(s, j):
-    @pl.when(j == 2)
-    def _():
-        s[pl.ds(SHARD - 2 * VT, HALF - SHARD), :] = jnp.full((HALF - SHARD, TB), -jnp.inf, F32)
-
-    @pl.when(j == 4)
-    def _():
-        s[pl.ds(HALF + SHARD - 4 * VT, HALF - SHARD), :] = jnp.full((HALF - SHARD, TB), -jnp.inf, F32)
+    for tile, at in ((2, SHARD - 2 * VT), (4, HALF + SHARD - 4 * VT)):
+        rows = pl.ds(at, HALF - SHARD)
+        s[rows, :] = jnp.where(j == tile, -jnp.inf, s[rows, :])
 
 
 AG_PATHS = ([(0, a, 0, D) for a in range(3)] + [(2, 0, 0, D), (4, 1, 0, D), (1, 2, 0, D)]
@@ -179,7 +177,6 @@
         return dot_last(e_v[pl.ds(off, VT), :], hn_s[pl.ds(tok, TB), :])
 
     def proc(q, s):
-        mask_pads(s, lax.rem(q, NT))
         blk = lax.div(q, NT)
         s3 = s[...].reshape(VT // 8, 8, TB)
         m8 = st[blk, 0]
@@ -197,8 +194,10 @@
             def _(units=units):
                 arrive(units)
         s1[...] = sdot(q + 1)
+        mask_pads(s0, lax.rem(q, NT))
         proc(q, s0)
         s0[...] = sdot(jnp.minimum(q + 2, NQ - 1))
+        mask_pads(s1, lax.rem(q + 1, NT))
         proc(q + 1, s1)
         return carry
 
@@ -269,7 +268,7 @@
 
 
 def bwd_kernel(hn_ref, e_ref, lse_ref, lab_ref, dh_ref, g_ref, l_ref,
-               e_v, hn_s, s0, s1, g0, g1, dh, ra, rb, rc, csem, gsem, ssem, rsem):
+               e_v, hn_s, s0, s1, g_s, dh, ra, rb, rc, csem, gsem, ssem, rsem):
     me = lax.axis_index('fsdp')
     nbr = [peer_of(me, 1 << a) for a in range(3)]
     barrier_with(nbr)
@@ -308,50 +307,48 @@
 
     iota = lax.broadcasted_iota(jnp.int32, (VT, TB), 0)
 
-    def g_copy(q, g, k):
-        blk, off = place(q)
-        return pltpu.make_async_copy(g, g_ref.at[pl.ds(off, VT), pl.ds(pl.multiple_of(blk * TB, TB), TB)], gsem.at[k])
-
-    def proc(q, s, g, k):
-        blk, off = place(q)
-        mask_pads(s, lax.rem(q, NT))
-
-        @pl.when(q >= 2)
-        def _():
-            g_copy(q, g, k).wait()
+    def g_copy(i, k):
+        blk, off = place(2 * i + k)
+        at = 2 * lax.rem(i, 2) + k
+        return pltpu.make_async_copy(g_s.at[at], g_ref.at[pl.ds(off, VT), pl.ds(pl.multiple_of(blk * TB, TB), TB)], gsem.at[at])
+
+    def proc(i, k, s):
+        blk, off = place(2 * i + k)
+        mask_pads(s, lax.rem(2 * i + k, NT))
         w = s[...] - lse_ref[blk]
         hit = iota == (lab_ref[blk] - off)
         p = jnp.exp2(w * LOG2E - 13.0)
         gv = (p - jnp.where(hit, 2.0 ** -13, 0.0)).astype(BF)
         l_ref[...] += jnp.where(hit, w, 0.0).reshape(VT // 8, 8, TB).sum(0)
-        g[...] = gv
+        g_s[2 * lax.rem(i, 2) + k] = gv
         rows = pl.ds(pl.multiple_of(blk * TB, TB), TB)
         dh[rows, :] += dot_first(gv, e_v[pl.ds(off, VT), :])
-
-    def after(q, g, k):
-        g_copy(q, g, k).start()
-        for i in range(NB):
-            @pl.when(q == i * NT + NT - 1)
-            def _(i=i):
-                finish(NB - 1 - i)
 
     load_e.wait()
     load_h.wait()
     s0[...] = sdot(0)
 
     def body(i, carry):
-        q = 2 * i
-        s1[...] = sdot(q + 1)
-        proc(q, s0, g0, 0)
-        after(q, g0, 0)
-        s0[...] = sdot(jnp.minimum(q + 2, NQ - 1))
-        proc(q + 1, s1, g1, 1)
-        after(q + 1, g1, 1)
+        @pl.when(i >= 2)
+        def _():
+            g_copy(i - 2, 0).wait()
+            g_copy(i - 2, 1).wait()
+        s1[...] = sdot(2 * i + 1)
+        proc(i, 0, s0)
+        s0[...] = sdot(jnp.minimum(2 * i + 2, NQ - 1))
+        proc(i, 1, s1)
+        g_copy(i, 0).start()
+        g_copy(i, 1).start()
+        for b in range(NB):
+            @pl.when(i == (b * NT + NT - 1) // 2)
+            def _(b=b):
+                finish(NB - 1 - b)
         return carry
 
     lax.fori_loop(0, NQ // 2, body, 0)
-    g_copy(NQ - 2, g0, 0).wait()
-    g_copy(NQ - 1, g1, 1).wait()
+    for i in (NQ // 2 - 2, NQ // 2 - 1):
+        g_copy(i, 0).wait()
+        g_copy(i, 1).wait()
     dh_ref[...] = dh[pl.ds(0, TOK), :]
     for k in range(len(RS_LIST)):
         piece(k).wait_send()
@@ -363,9 +360,9 @@
         bwd_kernel, in_specs=[ANY, ANY, VMEM, VMEM], out_specs=[VMEM, ANY, VMEM],
         out_shape=[jax.ShapeDtypeStruct((TOK, D), F32), jax.ShapeDtypeStruct((VP, GT), BF), jax.ShapeDtypeStruct((8, TB), F32)],
         scratch_shapes=[pltpu.VMEM((VP, D), BF), pltpu.VMEM((GT, D), BF), pltpu.VMEM((VT, TB), F32), pltpu.VMEM((VT, TB), F32),
-                        pltpu.VMEM((VT, TB), BF), pltpu.VMEM((VT, TB), BF), pltpu.VMEM((GT, D), F32),
+                        pltpu.VMEM((4, VT, TB), BF), pltpu.VMEM((GT, D), F32),
                         pltpu.VMEM((6, UNIT, 256), F32), pltpu.VMEM((6, UNIT, D), F32), pltpu.VMEM((6, UNIT, D), F32),
-                        pltpu.SemaphoreType.DMA((2,)), pltpu.SemaphoreType.DMA((2,)),
+                        pltpu.SemaphoreType.DMA((2,)), pltpu.SemaphoreType.DMA((4,)),
                         pltpu.SemaphoreType.DMA((n,)), pltpu.SemaphoreType.DMA((n,))],
         compiler_params=params(2), name='head_bwd')(hn_all, e_loc, lse, lab)
 
@@ -382,7 +379,6 @@
 
 
 def embed_grad(g, hn_all, rows, dx, scale):
-    import functools
     n = NB * CAP
     return pl.pallas_call(
         functools.partial(de_kernel, scale), grid=(VP // DE_T,),
@@ -394,23 +390,112 @@
         name='embed_grad')(g, hn_all, rows, dx)
 
 
-def rms_apply(values, gain_vec):
-    inv_rms = lax.rsqrt(jnp.mean(values * values, axis=-1, keepdims=True) + NORM_EPS)
-    return (values * inv_rms * gain_vec).astype(BF), inv_rms
+def rms_inv(values):
+    return lax.rsqrt(jnp.mean(values * values, axis=-1, keepdims=True) + NORM_EPS)
 
 
 def rms_backward(values, inv_rms, gain_vec, grad_out):
     scaled = grad_out * gain_vec
     return inv_rms * scaled - values * (inv_rms ** 3) * jnp.mean(scaled * values, axis=-1, keepdims=True)
+
+
+FT = 768
+NF = FF // FT
+
+
+def mlp_fwd_kernel(x_ref, gm_ref, gf_ref, wgu_ref, wd_ref, a_ref, gu_ref, q_ref, h_ref, hn_ref, acc):
+    f = pl.program_id(0)
+
+    @pl.when(f == 0)
+    def _():
+        x = x_ref[...].astype(F32) * EMB_SCALE
+        a_ref[...] = (x * rms_inv(x) * gm_ref[...]).astype(BF)
+        acc[...] = jnp.zeros_like(acc)
+    gu = dot_plain(a_ref[...], wgu_ref[...]).astype(BF)
+    gu_ref[...] = gu
+    g, u = gu[:, :FT].astype(F32), gu[:, FT:].astype(F32)
+    q = (g * jax.nn.sigmoid(g) * u).astype(BF)
+    q_ref[...] = q
+    acc[...] += dot_plain(q, wd_ref[...])
+
+    @pl.when(f == NF - 1)
+    def _():
+        x = x_ref[...].astype(F32) * EMB_SCALE
+        h = (x + acc[...].astype(BF).astype(F32)).astype(BF)
+        h_ref[...] = h
+        h = h.astype(F32)
+        hn_ref[...] = (h * rms_inv(h) * gf_ref[...]).astype(BF)
+
+
+def whole(shape):
+    return pl.BlockSpec(shape, lambda f: (0, 0))
+
+
+def mlp_forward(x, gain_mlp, gain_final, w_gu, w_down):
+    tok = jax.ShapeDtypeStruct((TOK, D), BF)
+    return pl.pallas_call(
+        mlp_fwd_kernel, grid=(NF,),
+        in_specs=[whole((TOK, D)), whole((1, D)), whole((1, D)), pl.BlockSpec((D, 2 * FT), lambda f: (0, f)),
+                  pl.BlockSpec((FT, D), lambda f: (f, 0))],
+        out_specs=[whole((TOK, D)), pl.BlockSpec((TOK, 2 * FT), lambda f: (0, f)), pl.BlockSpec((TOK, FT), lambda f: (0, f)),
+                   whole((TOK, D)), whole((TOK, D))],
+        out_shape=[tok, jax.ShapeDtypeStruct((TOK, 2 * FF), BF), jax.ShapeDtypeStruct((TOK, FF), BF), tok, tok],
+        scratch_shapes=[pltpu.VMEM((TOK, D), F32)],
+        compiler_params=pltpu.CompilerParams(vmem_limit_bytes=40 * 2 ** 20), name='mlp_fwd')(x, gain_mlp, gain_final, w_gu, w_down)
+
+
+def mlp_bwd_kernel(dh_ref, h_ref, x_ref, a_ref, gu_ref, q_ref, gm_ref, gf_ref, wgu_ref, wd_ref,
+                   dd_ref, dgu_ref, dx_ref, dh_s, dm_s, dn):
+    f = pl.program_id(0)
+
+    @pl.when(f == 0)
+    def _():
+        h = h_ref[...].astype(F32)
+        dh = rms_backward(h, rms_inv(h), gf_ref[...], dh_ref[...])
+        dh_s[...] = dh
+        dm_s[...] = dh.astype(BF)
+        dn[...] = jnp.zeros_like(dn)
+    dm = dm_s[...]
+    dd_ref[...] = dot_first(q_ref[...], dm)
+    dq = dot_last(dm, wd_ref[...])
+    g, u = gu_ref[:, :FT].astype(F32), gu_ref[:, FT:].astype(F32)
+    sig = jax.nn.sigmoid(g)
+    dg = (dq * u * sig * (1.0 + g * (1.0 - sig))).astype(BF)
+    du = (dq * g * sig).astype(BF)
+    a = a_ref[...]
+    dgu_ref[:, :FT] = dot_first(a, dg)
+    dgu_ref[:, FT:] = dot_first(a, du)
+    dn[...] += dot_last(dg, wgu_ref[:, :FT]) + dot_last(du, wgu_ref[:, FT:])
+
+    @pl.when(f == NF - 1)
+    def _():
+        x = x_ref[...].astype(F32) * EMB_SCALE
+        dx_ref[...] = (dh_s[...] + rms_backward(x, rms_inv(x), gm_ref[...], dn[...])).astype(BF)
+
+
+def mlp_backward(d_hid, h, x, a, gu, q, gain_mlp, gain_final, w_gu, w_down):
+    return pl.pallas_call(
+        mlp_bwd_kernel, grid=(NF,),
+        in_specs=[whole((TOK, D)), whole((TOK, D)), whole((TOK, D)), whole((TOK, D)), pl.BlockSpec((TOK, 2 * FT), lambda f: (0, f)),
+                  pl.BlockSpec((TOK, FT), lambda f: (0, f)), whole((1, D)), whole((1, D)),
+                  pl.BlockSpec((D, 2 * FT), lambda f: (0, f)), pl.BlockSpec((FT, D), lambda f: (f, 0))],
+        out_specs=[pl.BlockSpec((FT, D), lambda f: (f, 0)), pl.BlockSpec((D, 2 * FT), lambda f: (0, f)), whole((TOK, D))],
+        out_shape=[jax.ShapeDtypeStruct((FF, D), F32), jax.ShapeDtypeStruct((D, 2 * FF), F32), jax.ShapeDtypeStruct((TOK, D), BF)],
+        scratch_shapes=[pltpu.VMEM((TOK, D), F32), pltpu.VMEM((TOK, D), BF), pltpu.VMEM((TOK, D), F32)],
+        compiler_params=pltpu.CompilerParams(vmem_limit_bytes=60 * 2 ** 20),
+        name='mlp_bwd')(d_hid, h, x, a, gu, q, gain_mlp, gain_final, w_gu, w_down)
+
+
+def join_parts(gate, up):
+    return jnp.concatenate([w[:, f * FT:(f + 1) * FT] for f in range(NF) for w in (gate, up)], 1)
 
 
 def solution(mesh):
     def local_step(ids_blk, lab_blk, emb_shard, gate_shard, up_shard, down_shard, gain_mlp, gain_final):
         me = lax.axis_index('fsdp')
         core, chip = me % 2, me // 2
-        scale = math.sqrt(D)
         both = lax.all_gather(jnp.concatenate([ids_blk, lab_blk]), 'fsdp')
-        w_gu = lax.all_gather(jnp.concatenate([gate_shard, up_shard], 1), 'fsdp', tiled=True)
+        w_gu = lax.all_gather(join_parts(gate_shard, up_shard), 'fsdp', tiled=True)
         w_down = lax.all_gather(down_shard, 'fsdp', tiled=True)
         e_loc = pair_gather(emb_shard)
 
@@ -456,47 +541,34 @@
         x_bf = lookup(0, jnp.zeros((TOK, D), BF), 3)
         x_bf = lax.while_loop(lambda c: c[0] < rounds, lambda c: (c[0] + 1, lookup(c[0], c[1], 4)), (jnp.int32(1), x_bf))[1]
 
-        x_emb = x_bf.astype(F32) * scale
-        normed, inv_first = rms_apply(x_emb, gain_mlp)
-        gu = dot_plain(normed, w_gu).astype(BF)
-        gate, up_val = gu[:, :FF].astype(F32), gu[:, FF:].astype(F32)
-        hidden_act = (jax.nn.silu(gate) * up_val).astype(BF)
-        mlp_out = dot_plain(hidden_act, w_down).astype(BF)
-        hid32 = (x_emb + mlp_out.astype(F32)).astype(BF).astype(F32)
-        hid_norm, inv_final = rms_apply(hid32, gain_final)
+        gm, gf = gain_mlp[None, :], gain_final[None, :]
+        normed, gu, hidden_act, hid, hid_norm = mlp_forward(x_bf, gm, gf, w_gu, w_down)
 
         hn_all, lse = head_forward(hid_norm, e_loc)
         lab_pos = jnp.concatenate([lab_row[r, h * UNIT:(h + 1) * UNIT] for r, h in UNITS]).reshape(NB, 1, TB)
         d_hid, g_all, loss8 = head_backward(hn_all, e_loc, lse, lab_pos)
         loss = lax.psum(-jnp.sum(loss8), 'fsdp') * (1.0 / TOTAL)
 
-        d_hidden = rms_backward(hid32, inv_final, gain_final, d_hid)
-        d_mlp = d_hidden.astype(BF)
-        d_down = lax.psum_scatter(dot_first(hidden_act, d_mlp), 'fsdp', scatter_dimension=0, tiled=True)
-        d_act = dot_last(d_mlp, w_down)
-        sig = jax.nn.sigmoid(gate)
-        d_gate_pre = (d_act * up_val * sig * (1.0 + gate * (1.0 - sig))).astype(BF)
-        d_up_pre = (d_act * gate * sig).astype(BF)
-        d_gu_pre = jnp.concatenate([d_gate_pre, d_up_pre], 1)
-        d_gu = lax.psum_scatter(dot_first(normed, d_gu_pre), 'fsdp', scatter_dimension=0, tiled=True)
-        d_normed = dot_last(d_gu_pre, w_gu)
-        d_x = (d_hidden + rms_backward(x_emb, inv_first, gain_mlp, d_normed)).astype(BF)
+        d_down, d_gu, d_x = mlp_backward(d_hid, hid, x_bf, normed, gu, hidden_act, gm, gf, w_gu, w_down)
+        d_down = lax.psum_scatter(d_down, 'fsdp', scatter_dimension=0, tiled=True)
+        d_gu = lax.psum_scatter(d_gu, 'fsdp', scatter_dimension=0, tiled=True)
 
         def send_dx(rnd, cid):
             return swap(jnp.take(d_x, slot_tokens(rnd), axis=0, mode='clip').reshape(NB, CAP, D), cid).reshape(NB * CAP, D)
 
-        d_loc = embed_grad(g_all, hn_all, slot_rows(0)[None, :], send_dx(0, 5), scale)
+        d_loc = embed_grad(g_all, hn_all, slot_rows(0)[None, :], send_dx(0, 5), EMB_SCALE)
 
         def more(c):
             rnd, acc = c
             at = slot_rows(rnd)
-            add = jnp.where((at >= 0)[:, None], send_dx(rnd, 6).astype(F32) * scale, 0.0)
+            add = jnp.where((at >= 0)[:, None], send_dx(rnd, 6).astype(F32) * EMB_SCALE, 0.0)
             return rnd + 1, acc.at[jnp.maximum(at, 0)].add(add)
 
         d_loc = lax.while_loop(lambda c: c[0] < rounds, more, (jnp.int32(1), d_loc))[1]
         pairs = [(d, d ^ 1) for d in range(2 * NB)]
         d_embed = d_loc[:SHARD] + lax.ppermute(d_loc[HALF:HALF + SHARD], 'fsdp', pairs)
-        return loss, d_embed, d_gu[:, :FF], d_gu[:, FF:], d_down
+        d_gu = d_gu.reshape(-1, NF, 2, FT)
+        return loss, d_embed, d_gu[:, :, 0].reshape(-1, FF), d_gu[:, :, 1].reshape(-1, FF), d_down
 
     shard = P('fsdp', None)
     return jax.shard_map(local_step, mesh=mesh, in_specs=(shard,) * 6 + (P(), P()),

time: 601 us -> 580 us (0.965)
  matrix products: 57.1 us -> 0.36 us
  waiting for transfers between devices: 43.7 us -> 68.7 us
  local copies, waits for them, and re-layouts: 33.2 us -> 50.5 us
  other arithmetic: 23.5 us -> 16.3 us
    pallas_call x0 -> x2, Pallas kernels: none -> 40.1 us  [the longest x1 27.1 us: mlp_backward(): pl.pallas_call(mlp_bwd_kernel, grid=(NF,), in_specs=[whole((TOK, D)), who...]
    dot_general x4 -> x0, matrix products: 37.7 us -> none  [the longest x2 19.5 us: dot_first(): lax.dot_general(a, b, (((0,), (0,)), ((), ())), preferred_element_type=F32)]
    all_gather x1, waiting for transfers between devices: 0.02 us -> 23.2 us  [local_step(): w_gu = lax.all_gather(join_parts(gate_shard, up_shard), 'fsdp', tiled=True)]
    pallas_call x1, Pallas kernels: 149 us -> 128 us  [head_backward(): pl.pallas_call(bwd_kernel, in_specs=[ANY, ANY, VMEM, VMEM], out_specs=[VM...]
    reduce_scatter x2, waiting for transfers between devices: 24.9 us -> 44.8 us  [the longest x1 44.8 us: local_step(): d_down = lax.psum_scatter(d_down, 'fsdp', scatter_dimension=0, tiled=True)]
    dot_general x4 -> x2, matrix products: 19.4 us -> 0.36 us  [dot_plain(): lax.dot_general(a, b, (((1,), (0,)), ((), ())), preferred_element_type=F32)]
    all_gather x1, waiting for transfers between devices: 18.1 us -> 0.02 us  [local_step(): w_down = lax.all_gather(down_shard, 'fsdp', tiled=True)]
    pallas_call x1, Pallas kernels: 88.8 us -> 71 us  [head_forward(): pl.pallas_call(fwd_kernel, in_specs=[ANY, ANY], out_specs=[ANY, VMEM], ou...]
  transfers between devices with their start and end apart: 5 -> 5, of which waited for: 2 -> 2; matrix products, arithmetic and copies ran while one was open for 13% -> 10% of each run, Pallas kernels for 21% -> 22%
where the time goes in v2:
time: 580 us; the launch traced here: 572 us
  Pallas kernels  364 us (63%)
  waiting for transfers between devices  68.7 us (12%)
  blocking collectives  53.6 us (9%)
  local copies, waits for them, and re-layouts  50.5 us (9%)
  between operations  18 us (3%)
  other arithmetic  16.3 us (3%)
    pallas_call x1, Pallas kernels, head_backward(): pl.pallas_call(bwd_kernel, in_specs=[ANY, ANY, VMEM, VMEM], out_specs=[VM...  128 us
    pallas_call x1, Pallas kernels, head_forward(): pl.pallas_call(fwd_kernel, in_specs=[ANY, ANY], out_specs=[ANY, VMEM], ou...  71 us
    pallas_call x1, Pallas kernels, embed_grad(): pl.pallas_call(functools.partial(de_kernel, scale), grid=(VP // DE_T,), i...  58.7 us
    pallas_call x2, Pallas kernels, swap(): pl.pallas_call(swap_kernel, in_specs=[VMEM], out_specs=VMEM, out_shape=ja...  54.6 us
    reduce_scatter x1, waiting for transfers between devices, local_step(): d_down = lax.psum_scatter(d_down, 'fsdp', scatter_dimension=0, tiled=True)  44.8 us
    psum x1, blocking collectives, local_step(): loss = lax.psum(-jnp.sum(loss8), 'fsdp') * (1.0 / TOTAL)  38.7 us
    pallas_call x1, Pallas kernels, mlp_backward(): pl.pallas_call(mlp_bwd_kernel, grid=(NF,), in_specs=[whole((TOK, D)), who...  27.1 us
    all_gather x1, waiting for transfers between devices, local_step(): w_gu = lax.all_gather(join_parts(gate_shard, up_shard), 'fsdp', tiled=True)  23.2 us
  transfers between devices with their start and end apart: 5, of which 2 were waited for; matrix products, arithmetic and copies ran while one was open for 10% of the time, Pallas kernels for 22%

profile of v2, /device:TPU:0, one launch (start us, length us, event | category | flops | bytes accessed | tf_op | source)
XLA Modules:
  0.0 571.7 jit_solution(8058488599988224498)
XLA Ops:
  7.2 0.7 all-gather.7.cloned.1.call-update
  8.0 0.9 slice_dynamic-update-slice_fusion.7
  8.9 0.9 slice_dynamic-update-slice_fusion.6
  9.7 0.9 slice_dynamic-update-slice_fusion.5
  10.6 0.9 slice_dynamic-update-slice_fusion.4
  11.5 0.9 slice_dynamic-update-slice_fusion.3
  12.4 0.9 slice_dynamic-update-slice_fusion.2
  13.3 0.9 slice_dynamic-update-slice_fusion.1
  14.2 0.9 slice_dynamic-update-slice_fusion
  15.1 0.8 copy-done.12
  16.1 14.9 %all-gather.1 = s32[16,2,512]{2,1,0:T(2,128)S(1)} all-gather(s32[1,2,512]{2,1,0:T(2,128)S(1)} %add_bitcast_fusion.1), channel_id=2, replica_groups=mesh['fsdp'=16] {'fsdp'}, dimensions={0}, use_global_device_ids=true | all-gather | bytes 69632 | tf_op jit(solution)/shard_map/all_gather | solution.py:497
  31.2 0.4 convert_reduce_fusion
  31.5 0.6 reduce_max.9
  32.9 2.4 copy-done.1
  35.2 11.1 %pair_gather.1.e_ref = bf16[6400,768]{1,0:T(8,128)(2,1)} custom-call(bf16[3144,768]{1,0:T(8,128)(2,1)S(1)} %copy-done.1), custom_call_target="tpu_custom_call" | custom-call | tf_op jit(solution)/shard_map/pair_gather/pallas_call | solution.py:101
  46.5 0.6 gather_fusion.3
  47.4 0.2 fusion.12
  48.0 0.5 select_reduce_fusion.4
  48.5 9.5 %gather_fusion.4 = bf16[1024,768]{1,0:T(8,128)(2,1)S(1)} fusion(bf16[6400,768]{1,0:T(8,128)(2,1)} %pair_gather.1.e_ref, s32[1024]{0:T(1024)S(1)} %get-tuple-element.508), kind=kCustom, calls=%fused_computation.4 | custom fusion | bytes 3149824 | tf_op jit(solution)/shard_map/jit(_take)/gather | solution.py:535
  58.1 33.9 %swap.12 = bf16[8,128,768]{2,1,0:T(8,128)(2,1)S(1)} custom-call(bf16[8,128,768]{2,1,0:T(8,128)(2,1)S(1)} %bitcast.159), custom_call_target="tpu_custom_call" | custom-call | tf_op jit(solution)/shard_map/swap/pallas_call | solution.py:122
  92.1 2.0 gather_fusion.5
  94.4 1.0 broadcast_select_fusion.1
  95.5 0.5 while.29
  96.0 23.2 %all-gather.5.cloned.1.call-done.wgu_ref = bf16[768,6144]{1,0:T(8,128)(2,1)} async-done(((bf16[48,6144]{1,0:T(8,128)(2,1)}), bf16[768,6144]{1,0:T(8,128)(2,1)}) %all-gather.5.cloned.1.call-update) | async-done | bytes 9437200 | tf_op jit(solution)/shard_map/all_gather | solution.py:498
  119.2 2.3 copy-done
  121.5 13.0 %mlp_fwd.1 = (bf16[512,768]{1,0:T(8,128)(2,1)S(1)}, bf16[512,6144]{1,0:T(8,128)(2,1)}, bf16[512,3072]{1,0:T(8,128)(2,1)S(1)}, bf16[512,768]{1,0:T(8,128)(2,1)S(1)}, bf16[512,768]{1,0:T(8,128)(2,1)S(1)}) custom-call(bf16[512,768]{1,0:T(8,128)(2,1)} %get-tuple-element.357.x_ref, f32[1,768]{1,0:T(1,128)S(1)} %broadcast_in_dim.220.gm_ref, ...), custom_call_target="tpu_custom_call" | custom-call | tf_op jit(solution)/shard_map/mlp_fwd/pallas_call | solution.py:436
  134.5 1.7 copy-done.2
  136.3 0.9 copy-done.4
  137.1 0.9 copy-done.5
  138.0 0.9 copy-done.6
  138.9 71.0 %head_fwd.1 = (bf16[4096,768]{1,0:T(8,128)(2,1)}, f32[8,1,512]{2,1,0:T(1,128)}) custom-call(bf16[512,768]{1,0:T(8,128)(2,1)} %copy-done.6, bf16[6400,768]{1,0:T(8,128)(2,1)} %get-tuple-element.704), custom_call_target="tpu_custom_call" | custom-call | tf_op jit(solution)/shard_map/head_fwd/pallas_call | solution.py:244
  210.0 127.9 %head_bwd.1 = (f32[512,768]{1,0:T(8,128)}, bf16[6400,4096]{1,0:T(8,128)(2,1)}, f32[8,512]{1,0:T(8,128)}) custom-call(bf16[4096,768]{1,0:T(8,128)(2,1)} %get-tuple-element.359.hn_ref, bf16[6400,768]{1,0:T(8,128)(2,1)} %get-tuple-element.704, f32[8,1,512]{2,1,0:T(1,128)} %get-tuple-element.360.lse_ref, s32[8,1,512]{2,1,0:T(1,128)} %bitcast.172), custom_call_target="tpu_custom_call" | custom-call | tf_op jit(solution)/shard_map/head_bwd/pallas_call | solution.py:359
  337.9 27.1 %mlp_bwd.1 = (f32[3072,768]{1,0:T(8,128)}, f32[768,6144]{1,0:T(8,128)}, bf16[512,768]{1,0:T(8,128)(2,1)S(1)}) custom-call(f32[512,768]{1,0:T(8,128)} %get-tuple-element.363.dh_ref, bf16[512,768]{1,0:T(8,128)(2,1)} %copy-done.5, bf16[512,768]{1,0:T(8,128)(2,1)S(1)} %copy-done.11, bf16[512,768]{1,0:T(8,128)(2,1)} %copy-done.4, ...), custom_call_target="tpu_custom_call" | custom-call | tf_op jit(solution)/shard_map/mlp_bwd/pallas_call | solution.py:477
  365.1 0.4 select_reduce_fusion.3
  365.6 0.6 broadcast_add_fusion.2
  366.2 4.2 gather_fusion.6
  370.4 20.7 %swap.13 = bf16[8,128,768]{2,1,0:T(8,128)(2,1)S(1)} custom-call(bf16[8,128,768]{2,1,0:T(8,128)(2,1)S(1)} %bitcast.160), custom_call_target="tpu_custom_call" | custom-call | tf_op jit(solution)/shard_map/swap/pallas_call | solution.py:122
  391.1 1.1 copy-done.3
  392.2 58.7 %embed_grad.1 = f32[6400,768]{1,0:T(8,128)} custom-call(bf16[6400,4096]{1,0:T(8,128)(2,1)} %get-tuple-element.362.g_ref, bf16[4096,768]{1,0:T(8,128)(2,1)} %get-tuple-element.359.hn_ref, s32[1,1024]{1,0:T(1,128)} %bitcast.191, bf16[1024,768]{1,0:T(8,128)(2,1)} %bitcast.161), custom_call_target="tpu_custom_call" | custom-call | flops 50331648000 | bytes 72089600 | tf_op jit(solution)/shard_map/embed_grad/pallas_call | solution.py:383
  450.9 8.2 %slice.127 = f32[3144,768]{1,0:T(8,128)} slice(f32[6400,768]{1,0:T(8,128)} %get-tuple-element.369), slice={[3200:6344], [0:768]} | slice | bytes 19316736 | tf_op jit(solution)/shard_map/slice | solution.py:569
  459.1 0.6 reduce_sum.90
  460.4 38.7 %psum.7 = f32[]{:T(128)} all-reduce(f32[]{:T(128)S(6)} %neg.3), channel_id=1, replica_groups=mesh['fsdp'=16] {'fsdp'}, use_global_device_ids=true, to_apply=%region_8.9 | all-reduce | flops 1 | bytes 8 | tf_op jit(solution)/shard_map/psum | solution.py:550
  499.8 11.5 %slice_add_fusion = f32[3144,768]{1,0:T(8,128)} fusion(f32[3144,768]{1,0:T(8,128)} %collective-permute-done, f32[6400,768]{1,0:T(8,128)} %get-tuple-element.369), kind=kLoop, calls=%fused_computation.49 | loop fusion | flops 2414592 | bytes 28975104 | tf_op jit(solution)/shard_map/add | solution.py:569
  511.3 2.3 reshape.949
  513.6 3.3 slice_reduce_fusion
  516.9 0.9 copy.30
  517.8 0.9 copy.31
  518.8 44.8 %reduce-scatter.5.cloned.1.call-done = f32[192,768]{1,0:T(8,128)} async-done(((f32[3072,768]{1,0:T(8,128)}), f32[192,768]{1,0:T(8,128)}) %reduce-scatter.5.cloned.1.call-update) | async-done | bytes 589840 | tf_op jit(solution)/shard_map/reduce_scatter | solution.py:553
  (83 shorter events, 1.4 us)
Async XLA Ops:
  7.2 8.9 %copy-start.17 = (s32[1,512]{1,0:T(1,128)S(1)}, s32[1,512]{1,0:T(1,128)}, u32[]{:S(2)}) copy-start(s32[1,512]{1,0:T(1,128)} %param.13) | copy-start | bytes 6148
  7.2 8.9 %copy-start.18 = (s32[1,512]{1,0:T(1,128)S(1)}, s32[1,512]{1,0:T(1,128)}, u32[]{:S(2)}) copy-start(s32[1,512]{1,0:T(1,128)} %param.12) | copy-start | bytes 6148
  7.2 88.8 %all-gather.7.cloned.1.call-start = ((), (), s32[]{:S(2)}) async-start(), calls=%async_computation.3 | async-start | bytes 5013504 | tf_op jit(solution)/shard_map/all_gather | solution.py:499
  7.9 111.2 %all-gather.5.cloned.1.call-start = ((), (), s32[]{:S(2)}) async-start(), calls=%async_computation.2 | async-start | bytes 10027008 | tf_op jit(solution)/shard_map/all_gather | solution.py:498
  15.1 0.8 copy-start.12
  15.9 495.4 %reduce-scatter.3.cloned.1.call-start = ((), (), s32[]{:S(2)}) async-start(), calls=%async_computation.4 | async-start | bytes 20054016 | tf_op jit(solution)/shard_map/reduce_scatter | solution.py:554
  32.9 2.4 copy-start.1
  58.1 33.9 %copy-start.15 = (f32[768]{0:T(1024)S(1)}, f32[768]{0:T(1024)}, u32[]{:S(2)}) copy-start(f32[768]{0:T(1024)} %param.18) | copy-start | bytes 9220
  58.1 34.0 %copy-start.16 = (f32[768]{0:T(1024)S(1)}, f32[768]{0:T(1024)}, u32[]{:S(2)}) copy-start(f32[768]{0:T(1024)} %param.19) | copy-start | bytes 9220
  92.0 27.1 %copy-start.7 = (f32[1,768]{1,0:T(1,128)}, f32[1,768]{1,0:T(1,128)S(1)}, u32[]{:S(2)}) copy-start(f32[1,768]{1,0:T(1,128)S(1)} %broadcast_in_dim.220.gm_ref) | copy-start | bytes 9220
  92.1 27.1 %copy-start.8 = (f32[1,768]{1,0:T(1,128)}, f32[1,768]{1,0:T(1,128)S(1)}, u32[]{:S(2)}) copy-start(f32[1,768]{1,0:T(1,128)S(1)} %broadcast_in_dim.221.gf_ref) | copy-start | bytes 9220
  94.4 1.1 copy-start.14
  119.2 2.3 copy-start
  134.5 1.7 copy-start.2
  136.3 0.9 copy-start.4
  137.1 0.9 copy-start.5
  138.0 0.9 copy-start.6
  210.0 127.9 %copy-start.11 = (bf16[512,768]{1,0:T(8,128)(2,1)S(1)}, bf16[512,768]{1,0:T(8,128)(2,1)}, u32[]{:S(2)}) copy-start(bf16[512,768]{1,0:T(8,128)(2,1)} %get-tuple-element.357.x_ref) | copy-start | bytes 2359300
  365.0 198.6 %reduce-scatter.5.cloned.1.call-start = ((), (), s32[]{:S(2)}) async-start(), calls=%async_computation.5 | async-start | bytes 10027008 | tf_op jit(solution)/shard_map/reduce_scatter | solution.py:553
  391.1 1.1 copy-start.3
  450.9 8.2 %copy-start.13 = (f32[8,512]{1,0:T(8,128)S(1)}, f32[8,512]{1,0:T(8,128)}, u32[]{:S(2)}) copy-start(f32[8,512]{1,0:T(8,128)} %get-tuple-element.361) | copy-start | bytes 49156
  459.1 40.6 %collective-permute-start = (f32[3144,768]{1,0:T(8,128)}, f32[3144,768]{1,0:T(8,128)}, u32[]{:S(2)}, u32[]{:S(2)}) collective-permute-start(f32[3144,768]{1,0:T(8,128)} %slice.127), channel_id=1, source_target_pairs={{0,1},{1,0},{2,3},{3,2},{4,5},{5,4},{6,7},{7,6},{8,9},{9,8},{10,11... | collective-permute-start | bytes 28975112 | tf_op jit(solution)/shard_map/ppermute | solution.py:569
Sparse Core Ops, SparseCore 0:
  10.2 39.6 all-gather.6
  52.8 66.3 all-gather.4
  365.1 113.8 reduce-scatter.2
  484.2 79.3 reduce-scatter.4

commit v3 on v2

--- a/solution.py
+++ b/solution.py
@@ -14,6 +14,7 @@
 VMEM = pl.BlockSpec(memory_space=pltpu.VMEM)
 BF = jnp.bfloat16
 F32 = jnp.float32
+DMA = pltpu.SemaphoreType.DMA
 
 SHARD = 3144
 HALF = 3200
@@ -28,14 +29,44 @@
 VT = 1280
 NT = VP // VT
 NQ = NB * NT
-CAP = 128
+CAP = 96
+SLOTS = NB * CAP
 TOTAL = 8192
+NDEV = 2 * NB
+CHIP_ROWS = 2 * SHARD
+FF2 = 2 * FF
 EMB_SCALE = math.sqrt(D)
 
-BLOCKS = [[(0, 0), (0, 1)], [(2, 1), (1, 1)], [(4, 1), (1, 0)], [(4, 0), (2, 0)],
-          [(3, 1), (6, 1)], [(5, 1), (3, 0)], [(6, 0), (5, 0)], [(7, 0), (7, 1)]]
-UNITS = [u for b in BLOCKS for u in b]
+CUBE = range(NB)
+AXES = range(3)
+HALVES = range(2)
+
+
+def unit_list(text):
+    return [(int(r), 'ab'.index(h)) for r, h in zip(text[::2], text[1::2])]
+
+
+UNITS = unit_list('0a0b2b1b4b1a4a2a3b6b5b3a6a5a7a7b')
+BLOCKS = list(zip(UNITS[::2], UNITS[1::2]))
 POS = {u: i for i, u in enumerate(UNITS)}
+WAITS = {1: '2b1b4b', 2: '1a4a2a', 4: '3b6b5b', 5: '3a6a5a', 7: '7a7b'}
+ROW, COL = D // 3, D // 2
+CORNER = NB - 1
+STAR = [(1 << a, a, 0, D) for a in AXES]
+EDGE = [(CORNER - (1 << b), (b + 1 + j) % 3, j * COL, (j + 1) * COL) for b in (1, 0, 2) for j in HALVES]
+TIP = [(CORNER, a, a * ROW, (a + 1) * ROW) for a in AXES]
+SUMS = TIP + EDGE + STAR
+
+
+def landing(path):
+    s, a, lo, hi = path
+    t = s - (1 << a)
+    if s == CORNER:
+        return 0, a, 0
+    return (1, STAR_AT[t], lo) if t else (2, a, 0)
+
+
+STAR_AT = {1 << a: a for a in AXES}
 
 
 def dot_plain(a, b):
@@ -52,12 +83,10 @@
 
 def peer_of(me, r):
     p = me
-    if r & 1:
-        p = p + 2 - 4 * ((me // 2) % 2)
-    if r & 2:
-        p = p + 4 - 8 * ((me // 4) % 2)
-    if r & 4:
-        p = p + 8 - 16 * (me // 8)
+    for a in AXES:
+        if r >> a & 1:
+            step = 2 << a
+            p = p + step - step * (me // step % 2 * 2)
     return p
 
 
@@ -100,8 +129,8 @@
 def pair_gather(e_shard):
     return pl.pallas_call(
         pair_kernel, in_specs=[ANY], out_specs=ANY, out_shape=jax.ShapeDtypeStruct((VP, D), BF),
-        scratch_shapes=[pltpu.VMEM((SHARD, D), BF), pltpu.VMEM((HALF - SHARD, D), BF), pltpu.SemaphoreType.DMA((4,)),
-                        pltpu.SemaphoreType.DMA, pltpu.SemaphoreType.DMA],
+        scratch_shapes=[pltpu.VMEM((SHARD, D), BF), pltpu.VMEM((HALF - SHARD, D), BF), DMA((4,)),
+                        DMA, DMA],
         compiler_params=params(0, 16), name='pair_gather')(e_shard)
 
 
@@ -121,7 +150,7 @@
 def swap(rows, cid):
     return pl.pallas_call(
         swap_kernel, in_specs=[VMEM], out_specs=VMEM, out_shape=jax.ShapeDtypeStruct((NB, CAP, D), BF),
-        scratch_shapes=[pltpu.VMEM((NB, CAP, D), BF), pltpu.SemaphoreType.DMA((NB,)), pltpu.SemaphoreType.DMA((NB,))],
+        scratch_shapes=[pltpu.VMEM((NB, CAP, D), BF), DMA((NB,)), DMA((NB,))],
         compiler_params=params(cid, 16), name='swap')(rows)
 
 
@@ -131,8 +160,7 @@
         s[rows, :] = jnp.where(j == tile, -jnp.inf, s[rows, :])
 
 
-AG_PATHS = ([(0, a, 0, D) for a in range(3)] + [(2, 0, 0, D), (4, 1, 0, D), (1, 2, 0, D)]
-            + [(6, 0, 0, 256), (5, 1, 256, 512), (3, 2, 512, D)])
+AG_PATHS = [(0, a, 0, D) for a in AXES] + [(1 << (a + 1) % 3, a, 0, D) for a in AXES] + [(CORNER - (1 << a), a, lo, hi) for _, a, lo, hi in TIP]
 AG_LIST = [(s, h, a, lo, hi) for h in (1, 0) for (s, a, lo, hi) in AG_PATHS]
 
 
@@ -188,11 +216,10 @@
 
     def body(i, carry):
         q = 2 * i
-        for block, units in ((1, [(2, 1), (1, 1), (4, 1)]), (2, [(1, 0), (4, 0), (2, 0)]),
-                             (4, [(3, 1), (6, 1), (5, 1)]), (5, [(3, 0), (6, 0), (5, 0)]), (7, [(7, 0), (7, 1)])):
+        for block, units in WAITS.items():
             @pl.when(i == (block * NT - 1) // 2)
             def _(units=units):
-                arrive(units)
+                arrive(unit_list(units))
         s1[...] = sdot(q + 1)
         mask_pads(s0, lax.rem(q, NT))
         proc(q, s0)
@@ -211,27 +238,23 @@
         m = m8.max(0, keepdims=True)
         return m, (s8 * jnp.exp2((m8 - m) * LOG2E)).sum(0, keepdims=True)
 
-    for r in range(NB):
-        for h in range(2):
-            m, s = unit_stat((r, h))
-            stat[0, 2 * r:2 * r + 1, h * UNIT:(h + 1) * UNIT] = m
-            stat[0, 2 * r + 1:2 * r + 2, h * UNIT:(h + 1) * UNIT] = s
+    def stat_at(k, r):
+        return stat.at[k, k ^ r, 0:1], stat.at[k, k ^ r, 1:2]
+
+    for r in CUBE:
+        for h in HALVES:
+            for ref, val in zip(stat_at(0, r), unit_stat((r, h))):
+                ref[:, h * UNIT:(h + 1) * UNIT] = val
     sends = [remote(stat.at[0], stat.at[r], ssem2.at[r], rsem2.at[r], peers[r - 1]) for r in range(1, NB)]
     for c in sends:
         c.start()
     for c in sends:
         c.wait()
-    for r in range(NB):
-        ms = [stat[k, 2 * (k ^ r):2 * (k ^ r) + 1, :] for k in range(NB)]
-        ss = [stat[k, 2 * (k ^ r) + 1:2 * (k ^ r) + 2, :] for k in range(NB)]
-        top = ms[0]
-        for m in ms[1:]:
-            top = jnp.maximum(top, m)
-        tot = jnp.zeros_like(top)
-        for m, s in zip(ms, ss):
-            tot = tot + s * jnp.exp2((m - top) * LOG2E)
-        lse = top + jnp.log(tot)
-        for h in range(2):
+    for r in CUBE:
+        parts = [stat_at(k, r) for k in CUBE]
+        top = functools.reduce(jnp.maximum, [m[...] for m, _ in parts])
+        lse = top + jnp.log(sum(s[...] * jnp.exp2((m[...] - top) * LOG2E) for m, s in parts))
+        for h in HALVES:
             blk, at = POS[(r, h)] // 2, (POS[(r, h)] % 2) * UNIT
             lse_ref[blk, :, at:at + UNIT] = lse[:, h * UNIT:(h + 1) * UNIT]
     for k in range(len(AG_LIST)):
@@ -245,26 +268,13 @@
         fwd_kernel, in_specs=[ANY, ANY], out_specs=[ANY, VMEM],
         out_shape=[jax.ShapeDtypeStruct((GT, D), BF), jax.ShapeDtypeStruct((NB, 1, TB), F32)],
         scratch_shapes=[pltpu.VMEM((VP, D), BF), pltpu.VMEM((GT, D), BF), pltpu.VMEM((VT, TB), F32), pltpu.VMEM((VT, TB), F32),
-                        pltpu.VMEM((NB, 2, 8, TB), F32), pltpu.VMEM((NB, 16, TB), F32), pltpu.SemaphoreType.DMA((3,)),
-                        pltpu.SemaphoreType.DMA((n,)), pltpu.SemaphoreType.DMA((n,)),
-                        pltpu.SemaphoreType.DMA((NB,)), pltpu.SemaphoreType.DMA((NB,))],
+                        pltpu.VMEM((NB, 2, 8, TB), F32), pltpu.VMEM((NB, NB, 2, TB), F32), DMA((3,)),
+                        DMA((n,)), DMA((n,)),
+                        DMA((NB,)), DMA((NB,))],
         compiler_params=params(1), name='head_fwd')(hn, e_loc)
 
 
-RS_PATHS = [(7, 0, 0, 256), (7, 1, 256, 512), (7, 2, 512, D),
-            (5, 2, 0, 384), (5, 0, 384, D), (6, 1, 0, 384), (6, 2, 384, D), (3, 0, 0, 384), (3, 1, 384, D),
-            (1, 0, 0, D), (2, 1, 0, D), (4, 2, 0, D)]
-RS_LIST = [(s, h, a, lo, hi) for (s, a, lo, hi) in RS_PATHS for h in range(2)]
-
-
-def rs_place(k):
-    s, h, a, lo, hi = RS_LIST[k]
-    t = s ^ (1 << a)
-    if s == 7:
-        return 0, {6: 0, 5: 1, 3: 2}[t] * 2 + h, 0
-    if t:
-        return 1, {1: 0, 2: 1, 4: 2}[t] * 2 + h, lo
-    return 2, a * 2 + h, 0
+RS_LIST = [(p, h) for p in SUMS for h in HALVES]
 
 
 def bwd_kernel(hn_ref, e_ref, lse_ref, lab_ref, dh_ref, g_ref, l_ref,
@@ -281,21 +291,22 @@
     bufs = (ra, rb, rc)
 
     def piece(k):
-        s, h, a, lo, hi = RS_LIST[k]
+        (s, a, lo, hi), h = RS_LIST[k]
         src = dh.at[pl.ds(POS[(s, h)] * UNIT, UNIT), pl.ds(lo, hi - lo)]
-        b, i, c = rs_place(k)
-        return remote(src, bufs[b].at[i, :, pl.ds(c, hi - lo)], ssem.at[k], rsem.at[k], nbr[a])
+        b, i, c = landing(RS_LIST[k][0])
+        return remote(src, bufs[b].at[2 * i + h, :, pl.ds(c, hi - lo)], ssem.at[k], rsem.at[k], nbr[a])
 
     def finish(block):
-        for unit in BLOCKS[block]:
-            rows = pl.ds(POS[unit] * UNIT, UNIT)
-            for k, (s, h, a, lo, hi) in enumerate(RS_LIST):
-                if (s ^ (1 << a), h) == unit:
+        for r, half in BLOCKS[block]:
+            rows = pl.ds(POS[(r, half)] * UNIT, UNIT)
+            for k, (path, h) in enumerate(RS_LIST):
+                s, a, lo, hi = path
+                if (s ^ (1 << a), h) == (r, half):
                     piece(k).wait_recv()
-                    b, i, c = rs_place(k)
-                    dh[rows, lo:hi] += bufs[b][i, :, c:c + hi - lo]
-            for k, (s, h, a, lo, hi) in enumerate(RS_LIST):
-                if (s, h) == unit:
+                    b, i, c = landing(path)
+                    dh[rows, lo:hi] += bufs[b][2 * i + h, :, c:c + hi - lo]
+            for k, (path, h) in enumerate(RS_LIST):
+                if (path[0], h) == (r, half):
                     piece(k).start()
 
     def place(q):
@@ -362,32 +373,198 @@
         scratch_shapes=[pltpu.VMEM((VP, D), BF), pltpu.VMEM((GT, D), BF), pltpu.VMEM((VT, TB), F32), pltpu.VMEM((VT, TB), F32),
                         pltpu.VMEM((4, VT, TB), BF), pltpu.VMEM((GT, D), F32),
                         pltpu.VMEM((6, UNIT, 256), F32), pltpu.VMEM((6, UNIT, D), F32), pltpu.VMEM((6, UNIT, D), F32),
-                        pltpu.SemaphoreType.DMA((2,)), pltpu.SemaphoreType.DMA((4,)),
-                        pltpu.SemaphoreType.DMA((n,)), pltpu.SemaphoreType.DMA((n,))],
+                        DMA((2,)), DMA((4,)),
+                        DMA((n,)), DMA((n,))],
         compiler_params=params(2), name='head_bwd')(hn_all, e_loc, lse, lab)
 
 
-DE_T = 640
-
-
-def de_kernel(scale, g_ref, hn_ref, rows_ref, dx_ref, out_ref):
-    out_ref[...] = dot_plain(g_ref[...], hn_ref[...])
-    base = pl.program_id(0) * DE_T
-    iota = lax.broadcasted_iota(jnp.int32, (DE_T, NB * CAP), 0)
-    pick = jnp.where(iota == rows_ref[...] - base, 1.0, 0.0).astype(BF)
-    out_ref[...] += dot_plain(pick, dx_ref[...]) * scale
-
-
-def embed_grad(g, hn_all, rows, dx, scale):
-    n = NB * CAP
+ET = 320
+HT = HALF // ET
+NE = 2 * HT
+GD_ROWS = FF // (NDEV)
+GU_ROWS = D // (NDEV)
+SUM_ORDER = [CORNER] + [p[0] for p in EDGE[::2] + STAR[::-1]] + [0]
+
+
+def last_kernel(dd_ref, dgu_ref, dxs_ref, rows_ref, g_ref, hn_ref, l_ref,
+                de_ref, ogu_ref, odd_ref, loss_ref, pe_ref,
+                acc_d, acc_g, pair_d, pair_g, ra_d, ra_g, rb_d, rb_g, rc_d, rc_g, dxr, hn_s, g_s, ob, pb, lbuf,
+                psem, qsem, lsem, ssem, rsem, xs, xr, es, er, gsem, osem, csem, ls, lr):
+    me = lax.axis_index('fsdp')
+    core = me % 2
+    other = me + 1 - 2 * core
+    peers = [peer_of(me, r) for r in range(NB)]
+    far = [peers[r] + 1 - 2 * core for r in range(NB)]
+    everyone = peers[1:] + far
+    barrier_with(everyone)
+
+    lbuf[me] = sum(l_ref[:, k * 128:(k + 1) * 128] for k in range(TB // 128))
+    mats = ((dd_ref, acc_d, pair_d, GD_ROWS), (dgu_ref, acc_g, pair_g, GU_ROWS))
+
+    def pair_copy(r, m):
+        src, _, dst, n = mats[m]
+        return remote(src.at[pl.ds(pl.multiple_of(far[r] * n, n), n)], dst.at[r], psem.at[r, m], qsem.at[r, m], other)
+
+    def own_copy(r, m):
+        src, dst, _, n = mats[m]
+        return pltpu.make_async_copy(src.at[pl.ds(pl.multiple_of(peers[r] * n, n), n)], dst.at[r], lsem.at[r, m])
+
+    for r in SUM_ORDER:
+        for m in range(2):
+            pair_copy(r, m).start()
+            own_copy(r, m).start()
+    dx_copies = [remote(dxs_ref.at[pl.ds(r * CAP, CAP)], dxr.at[pl.ds(r * CAP, CAP)], xs.at[r], xr.at[r], peers[r])
+                 for r in range(1, NB)]
+    for c in dx_copies:
+        c.start()
+    loss_copies = [remote(lbuf.at[me], lbuf.at[me], ls.at[i], lr.at[i], p) for i, p in enumerate(everyone)]
+    for c in loss_copies:
+        c.start()
+    dx_own = pltpu.make_async_copy(dxs_ref.at[pl.ds(0, CAP)], dxr.at[pl.ds(0, CAP)], csem.at[0])
+    dx_own.start()
+    load_h = pltpu.make_async_copy(hn_ref, hn_s, csem.at[1])
+    load_h.start()
+
+    def odd(t):
+        return lax.rem(t, 2)
+
+    def g_load(t):
+        off = pl.multiple_of(lax.rem(t + HT, NE) * ET, ET)
+        return pltpu.make_async_copy(g_ref.at[pl.ds(off, ET)], g_s.at[odd(t)], gsem.at[odd(t)])
+
+    g_load(0).start()
+    bufs = ((ra_d, ra_g), (rb_d, rb_g), (rc_d, rc_g))
+    accs = (acc_d, acc_g)
+
+    def piece(k, m):
+        s, a, lo, hi = SUMS[k]
+        w = (1, 8)[m]
+        b, i, c = landing(SUMS[k])
+        return remote(accs[m].at[s, :, pl.ds(lo * w, (hi - lo) * w)], bufs[b][m].at[i, :, pl.ds(c * w, (hi - lo) * w)],
+                      ssem.at[k, m], rsem.at[k, m], peers[1 << a])
+
+    def pair_sum(r):
+        for m in range(2):
+            own_copy(r, m).wait()
+            pair_copy(r, m).wait_recv()
+            accs[m][r] += mats[m][2][r]
+
+    def pass_on(r):
+        for m in range(2):
+            w = (1, 8)[m]
+            for k, (s, a, lo, hi) in enumerate(SUMS):
+                if s ^ (1 << a) == r:
+                    piece(k, m).wait_recv()
+                    b, i, c = landing(SUMS[k])
+                    accs[m][r, :, lo * w:hi * w] += bufs[b][m][i, :, c * w:(c + hi - lo) * w]
+            for k, (s, a, lo, hi) in enumerate(SUMS):
+                if s == r:
+                    piece(k, m).start()
+
+    pair_sum(7)
+    pass_on(7)
+    for r in SUM_ORDER[1:]:
+        pair_sum(r)
+    dx_own.wait()
+    load_h.wait()
+    for c in dx_copies:
+        c.wait_recv()
+
+    def e_send(t):
+        return remote(ob.at[odd(t)], pe_ref.at[pl.ds(pl.multiple_of(t * ET, ET), ET)], es.at[t], er.at[t], other)
+
+    def e_out(t, n=ET):
+        at = pl.multiple_of((t - HT) * ET, ET)
+        return pltpu.make_async_copy(ob.at[odd(t), pl.ds(0, n)], de_ref.at[pl.ds(at, n)], osem.at[odd(t)])
+
+    def e_load(t):
+        return pltpu.make_async_copy(pe_ref.at[pl.ds(pl.multiple_of((t - HT) * ET, ET), ET)], pb, csem.at[2])
+
+    iota = lax.broadcasted_iota(jnp.int32, (ET, SLOTS), 0)
+    last = SHARD - (HT - 1) * ET
+
+    def body(t, carry):
+        for when, rs in ((5, SUM_ORDER[1:4]), (NE - 3, SUM_ORDER[4:7])):
+            @pl.when(t == when)
+            def _(rs=rs):
+                for r in rs:
+                    pass_on(r)
+
+        @pl.when((t >= 2) & (t < HT + 2))
+        def _():
+            e_send(t - 2).wait_send()
+
+        @pl.when(t >= HT + 2)
+        def _():
+            e_out(t - 2).wait()
+
+        @pl.when(t >= HT)
+        def _():
+            e_send(t - HT).wait_recv()
+            e_load(t).start()
+
+        @pl.when(t < NE - 1)
+        def _():
+            g_load(t + 1).start()
+        g_load(t).wait()
+        base = lax.rem(t + HT, NE) * ET
+        pick = jnp.where(iota == rows_ref[...] - base, 1.0, 0.0).astype(BF)
+        ob[odd(t)] = dot_plain(g_s[odd(t)], hn_s[...]) + dot_plain(pick, dxr[...]) * EMB_SCALE
+
+        @pl.when(t < HT)
+        def _():
+            e_send(t).start()
+
+        @pl.when(t >= HT)
+        def _():
+            e_load(t).wait()
+            ob[odd(t)] += pb[...]
+
+        @pl.when((t >= HT) & (t < NE - 1))
+        def _():
+            e_out(t).start()
+
+        @pl.when(t == NE - 1)
+        def _():
+            e_out(t, last).start()
+        return carry
+
+    lax.fori_loop(0, NE, body, 0)
+    for c in loss_copies:
+        c.wait()
+    tot = lbuf[0]
+    for i in range(1, NDEV):
+        tot = tot + lbuf[i]
+    loss_ref[...] = tot
+    pass_on(0)
+    ogu_ref[...] = acc_g[0]
+    odd_ref[...] = acc_d[0]
+    e_out(NE - 2).wait()
+    e_out(NE - 1, last).wait()
+    for c in dx_copies:
+        c.wait_send()
+    for m in range(2):
+        for r in SUM_ORDER:
+            pair_copy(r, m).wait_send()
+        for k in range(len(SUMS)):
+            piece(k, m).wait_send()
+
+
+def last_sums(d_down, d_gu, dxs, rows, g_all, hn_all, loss8):
+    n = len(SUMS)
+    scr = [pltpu.VMEM(s, F32) for s in ((NB, GD_ROWS, D), (NB, GU_ROWS, FF2), (NB, GD_ROWS, D), (NB, GU_ROWS, FF2),
+                                        (3, GD_ROWS, 256), (3, GU_ROWS, 2048), (3, GD_ROWS, D), (3, GU_ROWS, FF2),
+                                        (3, GD_ROWS, D), (3, GU_ROWS, FF2))]
+    scr += [pltpu.VMEM((SLOTS, D), BF), pltpu.VMEM((GT, D), BF), pltpu.VMEM((2, ET, GT), BF), pltpu.VMEM((2, ET, D), F32),
+            pltpu.VMEM((ET, D), F32), pltpu.VMEM((NDEV, 8, 128), F32)]
+    scr += [DMA((NB, 2)), DMA((NB, 2)), DMA((NB, 2)), DMA((n, 2)), DMA((n, 2)), DMA((NB,)), DMA((NB,)), DMA((HT,)), DMA((HT,)),
+            DMA((2,)), DMA((2,)), DMA((3,)), DMA((NDEV - 1,)), DMA((NDEV - 1,))]
     return pl.pallas_call(
-        functools.partial(de_kernel, scale), grid=(VP // DE_T,),
-        in_specs=[pl.BlockSpec((DE_T, GT), lambda j: (j, 0)), pl.BlockSpec((GT, D), lambda j: (0, 0)),
-                  pl.BlockSpec((1, n), lambda j: (0, 0)), pl.BlockSpec((n, D), lambda j: (0, 0))],
-        out_specs=pl.BlockSpec((DE_T, D), lambda j: (j, 0)), out_shape=jax.ShapeDtypeStruct((VP, D), F32),
-        compiler_params=pltpu.CompilerParams(vmem_limit_bytes=60 * 2 ** 20),
-        cost_estimate=pl.CostEstimate(flops=2 * VP * (GT + n) * D, bytes_accessed=VP * GT * 2 + VP * D * 4, transcendentals=0),
-        name='embed_grad')(g, hn_all, rows, dx)
+        last_kernel, in_specs=[ANY, ANY, ANY, VMEM, ANY, ANY, VMEM], out_specs=[ANY, VMEM, VMEM, VMEM, ANY],
+        out_shape=[jax.ShapeDtypeStruct((SHARD, D), F32), jax.ShapeDtypeStruct((GU_ROWS, FF2), F32),
+                   jax.ShapeDtypeStruct((GD_ROWS, D), F32), jax.ShapeDtypeStruct((8, 128), F32),
+                   jax.ShapeDtypeStruct((HALF, D), F32)],
+        scratch_shapes=scr, compiler_params=params(7, 63), name='last_sums')(d_down, d_gu, dxs, rows, g_all, hn_all, loss8)
 
 
 def rms_inv(values):
@@ -400,6 +577,7 @@
 
 
 FT = 768
+FT2 = 2 * FT
 NF = FF // FT
 
 
@@ -435,17 +613,17 @@
     tok = jax.ShapeDtypeStruct((TOK, D), BF)
     return pl.pallas_call(
         mlp_fwd_kernel, grid=(NF,),
-        in_specs=[whole((TOK, D)), whole((1, D)), whole((1, D)), pl.BlockSpec((D, 2 * FT), lambda f: (0, f)),
+        in_specs=[whole((TOK, D)), whole((1, D)), whole((1, D)), pl.BlockSpec((D, FT2), lambda f: (0, f)),
                   pl.BlockSpec((FT, D), lambda f: (f, 0))],
-        out_specs=[whole((TOK, D)), pl.BlockSpec((TOK, 2 * FT), lambda f: (0, f)), pl.BlockSpec((TOK, FT), lambda f: (0, f)),
+        out_specs=[whole((TOK, D)), pl.BlockSpec((TOK, FT2), lambda f: (0, f)), pl.BlockSpec((TOK, FT), lambda f: (0, f)),
                    whole((TOK, D)), whole((TOK, D))],
-        out_shape=[tok, jax.ShapeDtypeStruct((TOK, 2 * FF), BF), jax.ShapeDtypeStruct((TOK, FF), BF), tok, tok],
+        out_shape=[tok, jax.ShapeDtypeStruct((TOK, FF2), BF), jax.ShapeDtypeStruct((TOK, FF), BF), tok, tok],
         scratch_shapes=[pltpu.VMEM((TOK, D), F32)],
         compiler_params=pltpu.CompilerParams(vmem_limit_bytes=40 * 2 ** 20), name='mlp_fwd')(x, gain_mlp, gain_final, w_gu, w_down)
 
 
-def mlp_bwd_kernel(dh_ref, h_ref, x_ref, a_ref, gu_ref, q_ref, gm_ref, gf_ref, wgu_ref, wd_ref,
-                   dd_ref, dgu_ref, dx_ref, dh_s, dm_s, dn):
+def mlp_bwd_kernel(dh_ref, h_ref, x_ref, a_ref, gu_ref, q_ref, gm_ref, gf_ref, slot_ref, wgu_ref, wd_ref,
+                   dd_ref, dgu_ref, dx_ref, dxs_ref, dh_s, dm_s, dn):
     f = pl.program_id(0)
 
     @pl.when(f == 0)
@@ -470,20 +648,25 @@
     @pl.when(f == NF - 1)
     def _():
         x = x_ref[...].astype(F32) * EMB_SCALE
-        dx_ref[...] = (dh_s[...] + rms_backward(x, rms_inv(x), gm_ref[...], dn[...])).astype(BF)
-
-
-def mlp_backward(d_hid, h, x, a, gu, q, gain_mlp, gain_final, w_gu, w_down):
+        dx = (dh_s[...] + rms_backward(x, rms_inv(x), gm_ref[...], dn[...])).astype(BF)
+        dx_ref[...] = dx
+        pick = lax.broadcasted_iota(jnp.int32, (SLOTS, TOK), 0) == slot_ref[...]
+        dxs_ref[...] = dot_plain(jnp.where(pick, 1.0, 0.0).astype(BF), dx).astype(BF)
+
+
+def mlp_backward(d_hid, h, x, a, gu, q, gain_mlp, gain_final, slot, w_gu, w_down):
     return pl.pallas_call(
         mlp_bwd_kernel, grid=(NF,),
-        in_specs=[whole((TOK, D)), whole((TOK, D)), whole((TOK, D)), whole((TOK, D)), pl.BlockSpec((TOK, 2 * FT), lambda f: (0, f)),
-                  pl.BlockSpec((TOK, FT), lambda f: (0, f)), whole((1, D)), whole((1, D)),
-                  pl.BlockSpec((D, 2 * FT), lambda f: (0, f)), pl.BlockSpec((FT, D), lambda f: (f, 0))],
-        out_specs=[pl.BlockSpec((FT, D), lambda f: (f, 0)), pl.BlockSpec((D, 2 * FT), lambda f: (0, f)), whole((TOK, D))],
-        out_shape=[jax.ShapeDtypeStruct((FF, D), F32), jax.ShapeDtypeStruct((D, 2 * FF), F32), jax.ShapeDtypeStruct((TOK, D), BF)],
+        in_specs=[whole((TOK, D)), whole((TOK, D)), whole((TOK, D)), whole((TOK, D)), pl.BlockSpec((TOK, FT2), lambda f: (0, f)),
+                  pl.BlockSpec((TOK, FT), lambda f: (0, f)), whole((1, D)), whole((1, D)), whole((1, TOK)),
+                  pl.BlockSpec((D, FT2), lambda f: (0, f)), pl.BlockSpec((FT, D), lambda f: (f, 0))],
+        out_specs=[pl.BlockSpec((FT, D), lambda f: (f, 0)), pl.BlockSpec((D, FT2), lambda f: (0, f)), whole((TOK, D)),
+                   whole((SLOTS, D))],
+        out_shape=[jax.ShapeDtypeStruct((FF, D), F32), jax.ShapeDtypeStruct((D, FF2), F32), jax.ShapeDtypeStruct((TOK, D), BF),
+                   jax.ShapeDtypeStruct((SLOTS, D), BF)],
         scratch_shapes=[pltpu.VMEM((TOK, D), F32), pltpu.VMEM((TOK, D), BF), pltpu.VMEM((TOK, D), F32)],
         compiler_params=pltpu.CompilerParams(vmem_limit_bytes=60 * 2 ** 20),
-        name='mlp_bwd')(d_hid, h, x, a, gu, q, gain_mlp, gain_final, w_gu, w_down)
+        name='mlp_bwd')(d_hid, h, x, a, gu, q, gain_mlp, gain_final, slot, w_gu, w_down)
 
 
 def join_parts(gate, up):
@@ -504,9 +687,9 @@
         ids, labs = grp[:, 0], grp[:, 1]
 
         def local_row(v):
-            within = v % (2 * SHARD)
+            within = v % (CHIP_ROWS)
             row = jnp.where(within // SHARD == core, 0, HALF) + within % SHARD
-            return jnp.where(v // (2 * SHARD) == chip, row, -1)
+            return jnp.where(v // (CHIP_ROWS) == chip, row, -1)
 
         rows = local_row(ids)
         lab_row = local_row(labs)
@@ -514,26 +697,26 @@
         before = (jnp.arange(TOK)[:, None] < jnp.arange(TOK)[None, :]).astype(F32)
         rank = dot_plain(mine, before).astype(jnp.int32)
         slots = jnp.arange(CAP, dtype=jnp.int32)
-        own_chip = ids[0] // (2 * SHARD)
+        own_chip = ids[0] // (CHIP_ROWS)
         own_rel = jnp.bitwise_xor(own_chip, chip)
         is_rel = own_rel[None, :] == jnp.arange(NB)[:, None]
         own_rank_all = dot_plain(is_rel.astype(F32), before)
         own_rank = jnp.sum(jnp.where(is_rel, own_rank_all, 0.0), 0).astype(jnp.int32)
-        counts = jnp.sum((both[:, 0] // (2 * SHARD))[:, None, :] == jnp.arange(NB)[None, :, None], axis=-1)
+        counts = jnp.sum((both[:, 0] // (CHIP_ROWS))[:, None, :] == jnp.arange(NB)[None, :, None], axis=-1)
         rounds = (jnp.max(counts) + CAP - 1) // CAP
 
         def slot_rows(rnd):
             want = (rows[:, None, :] >= 0) & (rank[:, None, :] - rnd * CAP == slots[None, :, None])
             got = jnp.sum(jnp.where(want, rows[:, None, :] + 1, 0), axis=-1) - 1
-            return got.reshape(NB * CAP)
+            return got.reshape(SLOTS)
 
         def slot_tokens(rnd):
             want = is_rel[:, None, :] & (own_rank[None, None, :] - rnd * CAP == slots[None, :, None])
-            return jnp.sum(jnp.where(want, jnp.arange(TOK)[None, None, :], 0), axis=-1).reshape(NB * CAP)
+            return jnp.sum(jnp.where(want, jnp.arange(TOK)[None, None, :], 0), axis=-1).reshape(SLOTS)
 
         def lookup(rnd, x, cid):
             out = jnp.take(e_loc, jnp.maximum(slot_rows(rnd), 0), axis=0, mode='clip').reshape(NB, CAP, D)
-            got = swap(out, cid).reshape(NB * CAP, D)
+            got = swap(out, cid).reshape(SLOTS, D)
             here = own_rank // CAP == rnd
             at = jnp.where(here, own_rel * CAP + own_rank % CAP, 0)
             return jnp.where(here[:, None], jnp.take(got, at, axis=0, mode='clip'), x)
@@ -547,26 +730,22 @@
         hn_all, lse = head_forward(hid_norm, e_loc)
         lab_pos = jnp.concatenate([lab_row[r, h * UNIT:(h + 1) * UNIT] for r, h in UNITS]).reshape(NB, 1, TB)
         d_hid, g_all, loss8 = head_backward(hn_all, e_loc, lse, lab_pos)
-        loss = lax.psum(-jnp.sum(loss8), 'fsdp') * (1.0 / TOTAL)
-
-        d_down, d_gu, d_x = mlp_backward(d_hid, hid, x_bf, normed, gu, hidden_act, gm, gf, w_gu, w_down)
-        d_down = lax.psum_scatter(d_down, 'fsdp', scatter_dimension=0, tiled=True)
-        d_gu = lax.psum_scatter(d_gu, 'fsdp', scatter_dimension=0, tiled=True)
-
-        def send_dx(rnd, cid):
-            return swap(jnp.take(d_x, slot_tokens(rnd), axis=0, mode='clip').reshape(NB, CAP, D), cid).reshape(NB * CAP, D)
-
-        d_loc = embed_grad(g_all, hn_all, slot_rows(0)[None, :], send_dx(0, 5), EMB_SCALE)
+
+        slot = jnp.where(own_rank < CAP, own_rel * CAP + own_rank, -1)[None, :]
+        d_down, d_gu, d_x, dxs = mlp_backward(d_hid, hid, x_bf, normed, gu, hidden_act, gm, gf, slot, w_gu, w_down)
+        d_embed, d_gu, d_down, loss8, _ = last_sums(d_down, d_gu, dxs, slot_rows(0)[None, :], g_all, hn_all, loss8)
+        loss = -jnp.sum(loss8) * (1.0 / TOTAL)
 
         def more(c):
             rnd, acc = c
             at = slot_rows(rnd)
-            add = jnp.where((at >= 0)[:, None], send_dx(rnd, 6).astype(F32) * EMB_SCALE, 0.0)
-            return rnd + 1, acc.at[jnp.maximum(at, 0)].add(add)
-
-        d_loc = lax.while_loop(lambda c: c[0] < rounds, more, (jnp.int32(1), d_loc))[1]
-        pairs = [(d, d ^ 1) for d in range(2 * NB)]
-        d_embed = d_loc[:SHARD] + lax.ppermute(d_loc[HALF:HALF + SHARD], 'fsdp', pairs)
+            dx = swap(jnp.take(d_x, slot_tokens(rnd), axis=0, mode='clip').reshape(NB, CAP, D), 6).reshape(SLOTS, D)
+            add = jnp.where((at >= 0)[:, None], dx.astype(F32) * EMB_SCALE, 0.0)
+            part = jnp.zeros((VP, D), F32).at[jnp.maximum(at, 0)].add(add)
+            pairs = [(d, d ^ 1) for d in range(NDEV)]
+            return rnd + 1, acc + part[:SHARD] + lax.ppermute(part[HALF:HALF + SHARD], 'fsdp', pairs)
+
+        d_embed = lax.while_loop(lambda c: c[0] < rounds, more, (jnp.int32(1), d_embed))[1]
         d_gu = d_gu.reshape(-1, NF, 2, FT)
         return loss, d_embed, d_gu[:, :, 0].reshape(-1, FF), d_gu[:, :, 1].reshape(-1, FF), d_down
 

time: 580 us -> 530 us (0.914)
  Pallas kernels: 364 us -> 409 us
  waiting for transfers between devices: 68.7 us -> 29.9 us
  blocking collectives: 53.6 us -> 14.9 us
  other arithmetic: 16.3 us -> 4.69 us
    pallas_call x1, Pallas kernels: 58.7 us -> 120 us  [last_sums(): pl.pallas_call(last_kernel, in_specs=[ANY, ANY, ANY, VMEM, ANY, ANY, VMEM...]
    reduce_scatter x2 -> x0, waiting for transfers between devices: 44.8 us -> none  [the longest x1 44.8 us: local_step(): d_down = lax.psum_scatter(d_down, 'fsdp', scatter_dimension=0, tiled=True)]
    psum x1 -> x0, blocking collectives: 38.7 us -> none  [local_step(): loss = lax.psum(-jnp.sum(loss8), 'fsdp') * (1.0 / TOTAL)]
    pallas_call x2 -> x1, Pallas kernels: 54.6 us -> 23.9 us  [swap(): pl.pallas_call(swap_kernel, in_specs=[VMEM], out_specs=VMEM, out_shape=ja...]
    pallas_call x1, Pallas kernels: 27.1 us -> 43.1 us  [mlp_backward(): pl.pallas_call(mlp_bwd_kernel, grid=(NF,), in_specs=[whole((TOK, D)), who...]
    add x1 -> x0, other arithmetic: 11.5 us -> none  [local_step(): d_loc[:SHARD] + lax.ppermute(d_loc[HALF:HALF + SHARD], 'fsdp', pairs)]
    slice x1 -> x0, local copies, waits for them, and re-layouts: 8.19 us -> none  [local_step(): d_loc[HALF:HALF + SHARD]]
    unnamed x59 -> x57, local copies, waits for them, and re-layouts: 19.3 us -> 27.1 us
  transfers between devices with their start and end apart: 5 -> 2, of which waited for: 2 -> 1; matrix products, arithmetic and copies ran while one was open for 10% -> 4% of each run, Pallas kernels for 22% -> 6%
where the time goes in v3:
time: 530 us; the launch traced here: 522 us
  Pallas kernels  409 us (77%)
  local copies, waits for them, and re-layouts  45.5 us (9%)
  waiting for transfers between devices  29.9 us (6%)
  between operations  17.5 us (3%)
  blocking collectives  14.9 us (3%)
    pallas_call x1, Pallas kernels, head_backward(): pl.pallas_call(bwd_kernel, in_specs=[ANY, ANY, VMEM, VMEM], out_specs=[VM...  128 us
    pallas_call x1, Pallas kernels, last_sums(): pl.pallas_call(last_kernel, in_specs=[ANY, ANY, ANY, VMEM, ANY, ANY, VMEM...  120 us
    pallas_call x1, Pallas kernels, head_forward(): pl.pallas_call(fwd_kernel, in_specs=[ANY, ANY], out_specs=[ANY, VMEM], ou...  71 us
    pallas_call x1, Pallas kernels, mlp_backward(): pl.pallas_call(mlp_bwd_kernel, grid=(NF,), in_specs=[whole((TOK, D)), who...  43.1 us
    all_gather x1, waiting for transfers between devices, local_step(): w_gu = lax.all_gather(join_parts(gate_shard, up_shard), 'fsdp', tiled=True)  29.1 us
    unnamed x57, local copies, waits for them, and re-layouts  27.1 us
    pallas_call x1, Pallas kernels, swap(): pl.pallas_call(swap_kernel, in_specs=[VMEM], out_specs=VMEM, out_shape=ja...  23.9 us
    all_gather x1, blocking collectives, local_step(): both = lax.all_gather(jnp.concatenate([ids_blk, lab_blk]), 'fsdp')  14.9 us
  transfers between devices with their start and end apart: 2, of which 1 were waited for; matrix products, arithmetic and copies ran while one was open for 4% of the time, Pallas kernels for 6%

profile of v3, /device:TPU:0, one launch (start us, length us, event | category | flops | bytes accessed | tf_op | source)
XLA Modules:
  0.0 522.1 jit_solution(6474573110177695778)
XLA Ops:
  7.2 0.7 all-gather.7.cloned.1.call-update
  8.0 0.9 slice_dynamic-update-slice_fusion.7
  8.9 0.9 slice_dynamic-update-slice_fusion.6
  9.7 0.9 slice_dynamic-update-slice_fusion.5
  10.6 0.9 slice_dynamic-update-slice_fusion.4
  11.5 0.9 slice_dynamic-update-slice_fusion.3
  12.4 0.9 slice_dynamic-update-slice_fusion.2
  13.3 0.9 slice_dynamic-update-slice_fusion.1
  14.2 0.9 slice_dynamic-update-slice_fusion
  15.1 0.8 copy-done.10
  16.0 0.7 add_bitcast_fusion.1
  16.7 14.9 %all-gather.1 = s32[16,2,512]{2,1,0:T(2,128)S(1)} all-gather(s32[1,2,512]{2,1,0:T(2,128)S(1)} %add_bitcast_fusion.1), channel_id=2, replica_groups=mesh['fsdp'=16] {'fsdp'}, dimensions={0}, use_global_device_ids=true | all-gather | bytes 69632 | tf_op jit(solution)/shard_map/all_gather | solution.py:680
  31.7 0.2 and_select_fusion.2
  31.9 0.4 convert_reduce_fusion
  32.2 0.6 reduce_max.9
  33.6 0.1 stack.62
  33.7 0.6 gather_fusion.3
  34.6 0.2 fusion.14
  35.0 0.2 convolution_convert_fusion
  35.2 0.4 select_reduce_fusion.3
  35.6 0.7 sub.184.rows_ref
  36.3 2.4 copy-done.1
  38.7 9.9 %pair_gather.1.e_ref = bf16[6400,768]{1,0:T(8,128)(2,1)} custom-call(bf16[3144,768]{1,0:T(8,128)(2,1)S(1)} %copy-done.1), custom_call_target="tpu_custom_call" | custom-call | tf_op jit(solution)/shard_map/pair_gather/pallas_call | solution.py:130
  48.6 8.4 %gather_fusion.4 = bf16[768,768]{1,0:T(8,128)(2,1)S(1)} fusion(bf16[6400,768]{1,0:T(8,128)(2,1)} %pair_gather.1.e_ref, s32[1024]{0:T(1024)S(1)} %get-tuple-element.460), kind=kCustom, calls=%fused_computation.4 | custom fusion | bytes 2362368 | tf_op jit(solution)/shard_map/jit(_take)/gather | solution.py:718
  57.0 23.9 %swap.10 = bf16[8,96,768]{2,1,0:T(8,128)(2,1)S(1)} custom-call(bf16[8,96,768]{2,1,0:T(8,128)(2,1)S(1)} %bitcast.149), custom_call_target="tpu_custom_call" | custom-call | tf_op jit(solution)/shard_map/swap/pallas_call | solution.py:151
  81.0 2.0 gather_fusion.5
  83.3 0.6 compare_select_fusion.1.slot_ref
  83.9 0.1 broadcast_select_fusion.1
  84.0 0.3 while.28
  84.4 29.1 %all-gather.5.cloned.1.call-done.wgu_ref = bf16[768,6144]{1,0:T(8,128)(2,1)} async-done(((bf16[48,6144]{1,0:T(8,128)(2,1)}), bf16[768,6144]{1,0:T(8,128)(2,1)}) %all-gather.5.cloned.1.call-update) | async-done | bytes 9437200 | tf_op jit(solution)/shard_map/all_gather | solution.py:681
  113.5 2.3 copy-done
  115.8 13.0 %mlp_fwd.1 = (bf16[512,768]{1,0:T(8,128)(2,1)S(1)}, bf16[512,6144]{1,0:T(8,128)(2,1)}, bf16[512,3072]{1,0:T(8,128)(2,1)S(1)}, bf16[512,768]{1,0:T(8,128)(2,1)S(1)}, bf16[512,768]{1,0:T(8,128)(2,1)S(1)}) custom-call(bf16[512,768]{1,0:T(8,128)(2,1)S(1)} %get-tuple-element.303.x_ref, f32[1,768]{1,0:T(1,128)S(1)} %broadcast_in_dim.201.gm_ref, ...), custom_call_target="tpu_custom_call" | custom-call | tf_op jit(solution)/shard_map/mlp_fwd/pallas_call | solution.py:614
  128.8 1.6 copy-done.2
  130.4 0.9 copy-done.3
  131.3 0.9 copy-done.4
  132.2 0.9 copy-done.5
  133.1 71.0 %head_fwd.1 = (bf16[4096,768]{1,0:T(8,128)(2,1)}, f32[8,1,512]{2,1,0:T(1,128)}) custom-call(bf16[512,768]{1,0:T(8,128)(2,1)} %copy-done.5, bf16[6400,768]{1,0:T(8,128)(2,1)} %get-tuple-element.664), custom_call_target="tpu_custom_call" | custom-call | tf_op jit(solution)/shard_map/head_fwd/pallas_call | solution.py:267
  204.1 127.5 %head_bwd.1 = (f32[512,768]{1,0:T(8,128)}, bf16[6400,4096]{1,0:T(8,128)(2,1)}, f32[8,512]{1,0:T(8,128)}) custom-call(bf16[4096,768]{1,0:T(8,128)(2,1)} %get-tuple-element.305.hn_ref, bf16[6400,768]{1,0:T(8,128)(2,1)} %get-tuple-element.664, f32[8,1,512]{2,1,0:T(1,128)} %get-tuple-element.306.lse_ref, s32[8,1,512]{2,1,0:T(1,128)} %bitcast.162), custom_call_target="tpu_custom_call" | custom-call | tf_op jit(solution)/shard_map/head_bwd/pallas_call | solution.py:370
  331.7 43.1 %mlp_bwd.1 = (f32[3072,768]{1,0:T(8,128)}, f32[768,6144]{1,0:T(8,128)}, bf16[512,768]{1,0:T(8,128)(2,1)S(1)}, bf16[768,768]{1,0:T(8,128)(2,1)}) custom-call(f32[512,768]{1,0:T(8,128)} %get-tuple-element.307.dh_ref, bf16[512,768]{1,0:T(8,128)(2,1)} %copy-done.4, bf16[512,768]{1,0:T(8,128)(2,1)S(1)} %copy-done.9, bf16[512,768]{1,0:T(8,128)(2,1)} %copy-done.3, ...), custom_call_target="tpu_custom_call" | custom-call | tf_op jit(solution)/shard_map/mlp_bwd/pallas_call | solution.py:658
  374.8 120.3 %last_sums.1 = (f32[3144,768]{1,0:T(8,128)}, f32[48,6144]{1,0:T(8,128)}, f32[192,768]{1,0:T(8,128)}, f32[8,128]{1,0:T(8,128)}, f32[3200,768]{1,0:T(8,128)}) custom-call(f32[3072,768]{1,0:T(8,128)} %get-tuple-element.312.dd_ref, f32[768,6144]{1,0:T(8,128)} %get-tuple-element.313.dgu_ref, bf16[768,768]{1,0:T(8,128)(2,1)} %get-tuple-element.314.dxs_ref, ...), custom_call_target="tpu_custom_call" | custom-call | tf_op jit(solution)/shard_map/last_sums/pallas_call | solution.py:562
  495.1 1.3 reduce_sum.80
  497.0 0.2 while.29
  497.3 2.3 reshape.873
  499.5 3.3 slice_reduce_fusion
  502.9 0.9 copy.31
  503.8 0.9 copy.30
  504.7 8.2 %copy.88 = f32[3144,768]{1,0:T(8,128)} copy(f32[3144,768]{1,0:T(8,128)} %get-tuple-element.657) | data formatting | bytes 19316736
  513.0 0.8 copy.89
  (68 shorter events, 0.9 us)
Async XLA Ops:
  7.2 26.4 %copy-start.13 = (f32[768]{0:T(1024)S(1)}, f32[768]{0:T(1024)}, u32[]{:S(2)}) copy-start(f32[768]{0:T(1024)} %param.18) | copy-start | bytes 9220
  7.2 26.4 %copy-start.14 = (f32[768]{0:T(1024)S(1)}, f32[768]{0:T(1024)}, u32[]{:S(2)}) copy-start(f32[768]{0:T(1024)} %param.19) | copy-start | bytes 9220
  7.2 77.2 %all-gather.7.cloned.1.call-start = ((), (), s32[]{:S(2)}) async-start(), calls=%async_computation.1 | async-start | bytes 5013504 | tf_op jit(solution)/shard_map/all_gather | solution.py:682
  7.9 105.6 %all-gather.5.cloned.1.call-start = ((), (), s32[]{:S(2)}) async-start(), calls=%async_computation | async-start | bytes 10027008 | tf_op jit(solution)/shard_map/all_gather | solution.py:681
  15.1 0.8 copy-start.10
  33.6 79.9 %copy-start.6 = (f32[1,768]{1,0:T(1,128)}, f32[1,768]{1,0:T(1,128)S(1)}, u32[]{:S(2)}) copy-start(f32[1,768]{1,0:T(1,128)S(1)} %broadcast_in_dim.201.gm_ref) | copy-start | bytes 9220
  33.6 79.9 %copy-start.7 = (f32[1,768]{1,0:T(1,128)}, f32[1,768]{1,0:T(1,128)S(1)}, u32[]{:S(2)}) copy-start(f32[1,768]{1,0:T(1,128)S(1)} %broadcast_in_dim.202.gf_ref) | copy-start | bytes 9220
  36.3 2.4 copy-start.1
  83.3 0.7 copy-start.12
  84.3 44.5 %copy-start.8 = (bf16[512,768]{1,0:T(8,128)(2,1)}, bf16[512,768]{1,0:T(8,128)(2,1)S(1)}, u32[]{:S(2)}) copy-start(bf16[512,768]{1,0:T(8,128)(2,1)S(1)} %get-tuple-element.303.x_ref) | copy-start | bytes 2359300
  113.5 2.3 copy-start
  128.8 1.6 copy-start.2
  130.4 0.9 copy-start.3
  131.3 0.9 copy-start.4
  132.2 0.9 copy-start.5
  204.1 127.5 %copy-start.9 = (bf16[512,768]{1,0:T(8,128)(2,1)S(1)}, bf16[512,768]{1,0:T(8,128)(2,1)}, u32[]{:S(2)}) copy-start(bf16[512,768]{1,0:T(8,128)(2,1)} %copy-done.8) | copy-start | bytes 2359300
  504.7 8.2 %copy-start.11 = (f32[192,768]{1,0:T(8,128)S(1)}, f32[192,768]{1,0:T(8,128)}, u32[]{:S(2)}) copy-start(f32[192,768]{1,0:T(8,128)} %get-tuple-element.660) | copy-start | bytes 1769476
Sparse Core Ops, SparseCore 0:
  10.2 39.8 all-gather.6
  52.9 60.5 all-gather.4

commit v4 on v3

--- a/solution.py
+++ b/solution.py
@@ -35,6 +35,9 @@
 NDEV = 2 * NB
 CHIP_ROWS = 2 * SHARD
 FF2 = 2 * FF
+FT = 384
+FT2 = 2 * FT
+NF = FF // FT
 EMB_SCALE = math.sqrt(D)
 
 CUBE = range(NB)
@@ -79,6 +82,10 @@
 
 def dot_first(a, b):
     return lax.dot_general(a, b, (((0,), (0,)), ((), ())), preferred_element_type=F32)
+
+
+def one_hot(mask):
+    return jnp.where(mask, 1.0, 0.0).astype(BF)
 
 
 def peer_of(me, r):
@@ -378,207 +385,303 @@
         compiler_params=params(2), name='head_bwd')(hn_all, e_loc, lse, lab)
 
 
+def rms_inv(values):
+    return lax.rsqrt(jnp.mean(values * values, axis=-1, keepdims=True) + NORM_EPS)
+
+
+def rms_backward(values, inv_rms, gain_vec, grad_out):
+    scaled = grad_out * gain_vec
+    return inv_rms * scaled - values * (inv_rms ** 3) * jnp.mean(scaled * values, axis=-1, keepdims=True)
+
+
 ET = 320
 HT = HALF // ET
 NE = 2 * HT
-GD_ROWS = FF // (NDEV)
-GU_ROWS = D // (NDEV)
+GD = FF // NDEV
+GU = D // NDEV
 SUM_ORDER = [CORNER] + [p[0] for p in EDGE[::2] + STAR[::-1]] + [0]
 
 
-def last_kernel(dd_ref, dgu_ref, dxs_ref, rows_ref, g_ref, hn_ref, l_ref,
-                de_ref, ogu_ref, odd_ref, loss_ref, pe_ref,
-                acc_d, acc_g, pair_d, pair_g, ra_d, ra_g, rb_d, rb_g, rc_d, rc_g, dxr, hn_s, g_s, ob, pb, lbuf,
-                psem, qsem, lsem, ssem, rsem, xs, xr, es, er, gsem, osem, csem, ls, lr):
+def last_kernel(dhid_ref, h_ref, x_ref, a_ref, gu_ref, q_ref, wgu_ref, wd_ref, g_ref, hn_ref,
+                gm_ref, gf_ref, slot_ref, rows_ref, perm_ref, l_ref,
+                de_ref, ogate_ref, oup_ref, odd_ref, loss_ref, dx_ref, pe_ref,
+                acc_d, acc_g, pair_d, pair_g, ra_d, ra_g, rb_d, rb_g, rc_d, rc_g, dxs, dxr, lbuf,
+                pds, pdr, pgs, pgr, ssem, rsem, xs, xr, es, er, lsem, gsem, osem, csem, ls, lr, outsem):
     me = lax.axis_index('fsdp')
     core = me % 2
     other = me + 1 - 2 * core
-    peers = [peer_of(me, r) for r in range(NB)]
-    far = [peers[r] + 1 - 2 * core for r in range(NB)]
+    peers = [peer_of(me, r) for r in CUBE]
+    far = [p + 1 - 2 * core for p in peers]
     everyone = peers[1:] + far
     barrier_with(everyone)
 
     lbuf[me] = sum(l_ref[:, k * 128:(k + 1) * 128] for k in range(TB // 128))
-    mats = ((dd_ref, acc_d, pair_d, GD_ROWS), (dgu_ref, acc_g, pair_g, GU_ROWS))
-
-    def pair_copy(r, m):
-        src, _, dst, n = mats[m]
-        return remote(src.at[pl.ds(pl.multiple_of(far[r] * n, n), n)], dst.at[r], psem.at[r, m], qsem.at[r, m], other)
-
-    def own_copy(r, m):
-        src, dst, _, n = mats[m]
-        return pltpu.make_async_copy(src.at[pl.ds(pl.multiple_of(peers[r] * n, n), n)], dst.at[r], lsem.at[r, m])
-
-    for r in SUM_ORDER:
-        for m in range(2):
-            pair_copy(r, m).start()
-            own_copy(r, m).start()
-    dx_copies = [remote(dxs_ref.at[pl.ds(r * CAP, CAP)], dxr.at[pl.ds(r * CAP, CAP)], xs.at[r], xr.at[r], peers[r])
+    loss_copies = [remote(lbuf.at[me], lbuf.at[me], ls.at[i], lr.at[i], p) for i, p in enumerate(everyone)]
+    accs, pairs, sizes = (acc_d, acc_g), (pair_d, pair_g), (GD, GU)
+    bufs = ((ra_d, ra_g), (rb_d, rb_g), (rc_d, rc_g))
+    wide = (1, FF2 // D)
+
+    def block(m, r):
+        return pl.ds(pl.multiple_of(peers[r] // 2 * sizes[m], sizes[m]), sizes[m])
+
+    def piece(m, k):
+        s, a, lo, hi = SUMS[k]
+        w = wide[m]
+        b, i, c = landing(SUMS[k])
+        return remote(accs[m].at[block(m, s), pl.ds(lo * w, (hi - lo) * w)], bufs[b][m].at[i, :, pl.ds(c * w, (hi - lo) * w)],
+                      ssem.at[k, m], rsem.at[k, m], peers[1 << a])
+
+    def add_pair(m, r):
+        rows = block(m, r)
+        accs[m][rows, :] += pairs[m][rows, :]
+
+    def pass_on(m, r):
+        w = wide[m]
+        rows = block(m, r)
+        for k, (s, a, lo, hi) in enumerate(SUMS):
+            if s ^ (1 << a) == r:
+                piece(m, k).wait_recv()
+                b, i, c = landing(SUMS[k])
+                accs[m][rows, lo * w:hi * w] += bufs[b][m][i, :, c * w:(c + hi - lo) * w]
+        for k, (s, a, lo, hi) in enumerate(SUMS):
+            if s == r:
+                piece(m, k).start()
+
+    def odd(t):
+        return lax.rem(t, 2)
+
+    def mlp(x_s, p_s, dm_s, dgu_s, dh_s, dn, q_t, wd_t, gu_t, wgu_t, tg):
+        loads = [pltpu.make_async_copy(src, dst, csem.at[i]) for i, (src, dst) in
+                 enumerate(((dhid_ref, dh_s), (h_ref, x_s), (a_ref, dgu_s), (x_ref, x_s)))]
+        load_x = loads.pop()
+        for c in loads:
+            c.start()
+
+        def cols(f, n):
+            return pl.ds(pl.multiple_of(f * n, n), n)
+
+        def q_load(f):
+            return pltpu.make_async_copy(q_ref.at[:, cols(f, FT)], q_t.at[odd(f)], lsem.at[odd(f), 0])
+
+        def w_loads(f):
+            return [pltpu.make_async_copy(wd_ref.at[cols(f, FT)], wd_t.at[odd(f)], lsem.at[odd(f), 1]),
+                    pltpu.make_async_copy(gu_ref.at[:, cols(f, FT2)], gu_t.at[odd(f)], lsem.at[odd(f), 2]),
+                    pltpu.make_async_copy(wgu_ref.at[:, cols(f, FT2)], wgu_t.at[odd(f)], lsem.at[odd(f), 3])]
+
+        def d_send(f):
+            return remote(tg.at[odd(f), cols(1 - core, GD)], pair_d.at[cols(f, GD)],
+                          pds.at[f], pdr.at[f], other)
+
+        def g_send(f):
+            return remote(tg.at[odd(f)], pair_g.at[:, cols(f, FT2)],
+                          pgs.at[f], pgr.at[f], other)
+
+        q_load(0).start()
+        for c in w_loads(0):
+            c.start()
+        for c in loss_copies:
+            c.start()
+        for c in loads:
+            c.wait()
+        h = x_s[...].astype(F32)
+        dh = rms_backward(h, rms_inv(h), gf_ref[...], dh_s[...])
+        dh_s[...] = dh
+        dm_s[...] = dh.astype(BF)
+        dn[...] = jnp.zeros_like(dn)
+        pick = lax.broadcasted_iota(jnp.int32, (D, D), 0) == perm_ref[...]
+        p_s[...] = dot_plain(dgu_s[...], one_hot(pick)).astype(BF)
+        load_x.start()
+
+        def down(f, carry):
+            @pl.when(f < NF - 1)
+            def _():
+                q_load(f + 1).start()
+
+            @pl.when(f >= 2)
+            def _():
+                d_send(f - 2).wait_send()
+            q_load(f).wait()
+            tg[odd(f)] = dot_first(q_t[odd(f)], dm_s[...])
+            acc_d[cols(f, GD), :] = tg[odd(f), cols(core, GD)]
+            d_send(f).start()
+            return carry
+
+        def settle(send):
+            for f in range(NF):
+                send(f).wait_recv()
+            for f in (NF - 2, NF - 1):
+                send(f).wait_send()
+
+        lax.fori_loop(0, NF, down, 0)
+        settle(d_send)
+        add_pair(0, CORNER)
+        pass_on(0, CORNER)
+        for r in SUM_ORDER[1:]:
+            add_pair(0, r)
+
+        def gate_up(f, carry):
+            for when, rs in ((2, SUM_ORDER[1:4]), (NF - 1, SUM_ORDER[4:7])):
+                @pl.when(f == when)
+                def _(rs=rs):
+                    for r in rs:
+                        pass_on(0, r)
+
+            @pl.when(f < NF - 1)
+            def _():
+                for c in w_loads(f + 1):
+                    c.start()
+
+            @pl.when(f >= 2)
+            def _():
+                g_send(f - 2).wait_send()
+            for c in w_loads(f):
+                c.wait()
+            dq = dot_last(dm_s[...], wd_t[odd(f)])
+            g, u = gu_t[odd(f), :, :FT].astype(F32), gu_t[odd(f), :, FT:].astype(F32)
+            sig = jax.nn.sigmoid(g)
+            dgu_s[:, :FT] = (dq * u * sig * (1.0 + g * (1.0 - sig))).astype(BF)
+            dgu_s[:, FT:] = (dq * g * sig).astype(BF)
+            tg[odd(f)] = dot_first(p_s[:, FT:], dgu_s[...])
+            g_send(f).start()
+            acc_g[:, cols(f, FT2)] = dot_first(p_s[:, :FT], dgu_s[...])
+            dn[...] += dot_last(dgu_s[...], wgu_t[odd(f)])
+            return carry
+
+        lax.fori_loop(0, NF, gate_up, 0)
+        load_x.wait()
+        x = x_s[...].astype(F32) * EMB_SCALE
+        dx = (dh_s[...] + rms_backward(x, rms_inv(x), gm_ref[...], dn[...])).astype(BF)
+        dx_ref[...] = dx
+        pick = lax.broadcasted_iota(jnp.int32, (SLOTS, TOK), 0) == slot_ref[...]
+        dxs[...] = dot_plain(one_hot(pick), dx).astype(BF)
+        settle(g_send)
+
+    pl.run_scoped(mlp, *[pltpu.VMEM((TOK, D), BF)] * 4, *[pltpu.VMEM((TOK, D), F32)] * 2,
+                  *[pltpu.VMEM((2, *shape), BF) for shape in ((TOK, FT), (FT, D), (TOK, FT2), (D, FT2))], pltpu.VMEM((2, FT, D), F32))
+
+    dx_copies = [remote(dxs.at[pl.ds(r * CAP, CAP)], dxr.at[pl.ds(r * CAP, CAP)], xs.at[r], xr.at[r], peers[r])
                  for r in range(1, NB)]
+    add_pair(1, CORNER)
+    pass_on(1, CORNER)
     for c in dx_copies:
         c.start()
-    loss_copies = [remote(lbuf.at[me], lbuf.at[me], ls.at[i], lr.at[i], p) for i, p in enumerate(everyone)]
-    for c in loss_copies:
-        c.start()
-    dx_own = pltpu.make_async_copy(dxs_ref.at[pl.ds(0, CAP)], dxr.at[pl.ds(0, CAP)], csem.at[0])
-    dx_own.start()
-    load_h = pltpu.make_async_copy(hn_ref, hn_s, csem.at[1])
-    load_h.start()
-
-    def odd(t):
-        return lax.rem(t, 2)
-
-    def g_load(t):
-        off = pl.multiple_of(lax.rem(t + HT, NE) * ET, ET)
-        return pltpu.make_async_copy(g_ref.at[pl.ds(off, ET)], g_s.at[odd(t)], gsem.at[odd(t)])
-
-    g_load(0).start()
-    bufs = ((ra_d, ra_g), (rb_d, rb_g), (rc_d, rc_g))
-    accs = (acc_d, acc_g)
-
-    def piece(k, m):
-        s, a, lo, hi = SUMS[k]
-        w = (1, 8)[m]
-        b, i, c = landing(SUMS[k])
-        return remote(accs[m].at[s, :, pl.ds(lo * w, (hi - lo) * w)], bufs[b][m].at[i, :, pl.ds(c * w, (hi - lo) * w)],
-                      ssem.at[k, m], rsem.at[k, m], peers[1 << a])
-
-    def pair_sum(r):
-        for m in range(2):
-            own_copy(r, m).wait()
-            pair_copy(r, m).wait_recv()
-            accs[m][r] += mats[m][2][r]
-
-    def pass_on(r):
-        for m in range(2):
-            w = (1, 8)[m]
-            for k, (s, a, lo, hi) in enumerate(SUMS):
-                if s ^ (1 << a) == r:
-                    piece(k, m).wait_recv()
-                    b, i, c = landing(SUMS[k])
-                    accs[m][r, :, lo * w:hi * w] += bufs[b][m][i, :, c * w:(c + hi - lo) * w]
-            for k, (s, a, lo, hi) in enumerate(SUMS):
-                if s == r:
-                    piece(k, m).start()
-
-    pair_sum(7)
-    pass_on(7)
+    dxr[pl.ds(0, CAP)] = dxs[pl.ds(0, CAP)]
     for r in SUM_ORDER[1:]:
-        pair_sum(r)
-    dx_own.wait()
-    load_h.wait()
-    for c in dx_copies:
-        c.wait_recv()
-
-    def e_send(t):
-        return remote(ob.at[odd(t)], pe_ref.at[pl.ds(pl.multiple_of(t * ET, ET), ET)], es.at[t], er.at[t], other)
-
-    def e_out(t, n=ET):
-        at = pl.multiple_of((t - HT) * ET, ET)
-        return pltpu.make_async_copy(ob.at[odd(t), pl.ds(0, n)], de_ref.at[pl.ds(at, n)], osem.at[odd(t)])
-
-    def e_load(t):
-        return pltpu.make_async_copy(pe_ref.at[pl.ds(pl.multiple_of((t - HT) * ET, ET), ET)], pb, csem.at[2])
-
-    iota = lax.broadcasted_iota(jnp.int32, (ET, SLOTS), 0)
-    last = SHARD - (HT - 1) * ET
-
-    def body(t, carry):
-        for when, rs in ((5, SUM_ORDER[1:4]), (NE - 3, SUM_ORDER[4:7])):
-            @pl.when(t == when)
-            def _(rs=rs):
-                for r in rs:
-                    pass_on(r)
-
-        @pl.when((t >= 2) & (t < HT + 2))
-        def _():
-            e_send(t - 2).wait_send()
-
-        @pl.when(t >= HT + 2)
-        def _():
-            e_out(t - 2).wait()
-
-        @pl.when(t >= HT)
-        def _():
-            e_send(t - HT).wait_recv()
-            e_load(t).start()
-
-        @pl.when(t < NE - 1)
-        def _():
-            g_load(t + 1).start()
-        g_load(t).wait()
-        base = lax.rem(t + HT, NE) * ET
-        pick = jnp.where(iota == rows_ref[...] - base, 1.0, 0.0).astype(BF)
-        ob[odd(t)] = dot_plain(g_s[odd(t)], hn_s[...]) + dot_plain(pick, dxr[...]) * EMB_SCALE
-
-        @pl.when(t < HT)
-        def _():
-            e_send(t).start()
-
-        @pl.when(t >= HT)
-        def _():
-            e_load(t).wait()
-            ob[odd(t)] += pb[...]
-
-        @pl.when((t >= HT) & (t < NE - 1))
-        def _():
-            e_out(t).start()
-
-        @pl.when(t == NE - 1)
-        def _():
-            e_out(t, last).start()
-        return carry
-
-    lax.fori_loop(0, NE, body, 0)
+        add_pair(1, r)
+
+    def embed(hn_s, g_s, ob, pb):
+        load_h = pltpu.make_async_copy(hn_ref, hn_s, csem.at[0])
+        load_h.start()
+
+        def g_load(t):
+            off = pl.multiple_of(lax.rem(t + HT, NE) * ET, ET)
+            return pltpu.make_async_copy(g_ref.at[pl.ds(off, ET)], g_s.at[odd(t)], gsem.at[odd(t)])
+
+        def e_send(t):
+            return remote(ob.at[odd(t)], pe_ref.at[pl.ds(pl.multiple_of(t * ET, ET), ET)], es.at[t], er.at[t], other)
+
+        def e_out(t, n=ET):
+            at = pl.multiple_of((t - HT) * ET, ET)
+            return pltpu.make_async_copy(ob.at[odd(t), pl.ds(0, n)], de_ref.at[pl.ds(at, n)], osem.at[odd(t)])
+
+        def e_load(t):
+            return pltpu.make_async_copy(pe_ref.at[pl.ds(pl.multiple_of((t - HT) * ET, ET), ET)], pb, csem.at[1])
+
+        g_load(0).start()
+        load_h.wait()
+        for c in dx_copies:
+            c.wait_recv()
+        iota = lax.broadcasted_iota(jnp.int32, (ET, SLOTS), 0)
+        last = SHARD - (HT - 1) * ET
+
+        def body(t, carry):
+            for when, rs in ((HT - 2, SUM_ORDER[1:4]), (NE - 1, SUM_ORDER[4:7])):
+                @pl.when(t == when)
+                def _(rs=rs):
+                    for r in rs:
+                        pass_on(1, r)
+
+            @pl.when((t >= 2) & (t < HT + 2))
+            def _():
+                e_send(t - 2).wait_send()
+
+            @pl.when(t >= HT + 2)
+            def _():
+                e_out(t - 2).wait()
+
+            @pl.when(t >= HT)
+            def _():
+                e_send(t - HT).wait_recv()
+                e_load(t).start()
+
+            @pl.when(t < NE - 1)
+            def _():
+                g_load(t + 1).start()
+            g_load(t).wait()
+            base = lax.rem(t + HT, NE) * ET
+            pick = one_hot(iota == rows_ref[...] - base)
+            ob[odd(t)] = dot_plain(g_s[odd(t)], hn_s[...]) + dot_plain(pick, dxr[...]) * EMB_SCALE
+
+            @pl.when(t < HT)
+            def _():
+                e_send(t).start()
+
+            @pl.when(t >= HT)
+            def _():
+                e_load(t).wait()
+                ob[odd(t)] += pb[...]
+
+            @pl.when((t >= HT) & (t < NE - 1))
+            def _():
+                e_out(t).start()
+
+            @pl.when(t == NE - 1)
+            def _():
+                e_out(t, last).start()
+            return carry
+
+        lax.fori_loop(0, NE, body, 0)
+        e_out(NE - 2).wait()
+        e_out(NE - 1, last).wait()
+
+    pl.run_scoped(embed, pltpu.VMEM((GT, D), BF), pltpu.VMEM((2, ET, GT), BF), pltpu.VMEM((2, ET, D), F32), pltpu.VMEM((ET, D), F32))
     for c in loss_copies:
         c.wait()
     tot = lbuf[0]
     for i in range(1, NDEV):
         tot = tot + lbuf[i]
     loss_ref[...] = tot
-    pass_on(0)
-    ogu_ref[...] = acc_g[0]
-    odd_ref[...] = acc_d[0]
-    e_out(NE - 2).wait()
-    e_out(NE - 1, last).wait()
+    for m in HALVES:
+        pass_on(m, 0)
+    outs = [pltpu.make_async_copy(acc_d.at[block(0, 0)], odd_ref, gsem.at[0])]
+    for f in range(NF):
+        for i, out in enumerate((ogate_ref, oup_ref)):
+            part = acc_g.at[block(1, 0), pl.ds((2 * f + i) * FT, FT)]
+            outs.append(pltpu.make_async_copy(part, out.at[:, pl.ds(f * FT, FT)], outsem.at[f, i]))
+    for c in outs:
+        c.start()
+    for c in outs:
+        c.wait()
     for c in dx_copies:
         c.wait_send()
-    for m in range(2):
-        for r in SUM_ORDER:
-            pair_copy(r, m).wait_send()
+    for m in HALVES:
         for k in range(len(SUMS)):
-            piece(k, m).wait_send()
-
-
-def last_sums(d_down, d_gu, dxs, rows, g_all, hn_all, loss8):
+            piece(m, k).wait_send()
+
+
+def last_sums(*args):
     n = len(SUMS)
-    scr = [pltpu.VMEM(s, F32) for s in ((NB, GD_ROWS, D), (NB, GU_ROWS, FF2), (NB, GD_ROWS, D), (NB, GU_ROWS, FF2),
-                                        (3, GD_ROWS, 256), (3, GU_ROWS, 2048), (3, GD_ROWS, D), (3, GU_ROWS, FF2),
-                                        (3, GD_ROWS, D), (3, GU_ROWS, FF2))]
-    scr += [pltpu.VMEM((SLOTS, D), BF), pltpu.VMEM((GT, D), BF), pltpu.VMEM((2, ET, GT), BF), pltpu.VMEM((2, ET, D), F32),
-            pltpu.VMEM((ET, D), F32), pltpu.VMEM((NDEV, 8, 128), F32)]
-    scr += [DMA((NB, 2)), DMA((NB, 2)), DMA((NB, 2)), DMA((n, 2)), DMA((n, 2)), DMA((NB,)), DMA((NB,)), DMA((HT,)), DMA((HT,)),
-            DMA((2,)), DMA((2,)), DMA((3,)), DMA((NDEV - 1,)), DMA((NDEV - 1,))]
+    scr = [pltpu.VMEM(shape, F32) for shape in ((NB * GD, D), (NB * GU, FF2)) * 2 + (
+        (3, GD, ROW), (3, GU, ROW * FF2 // D)) + ((3, GD, D), (3, GU, FF2)) * 2]
+    scr += [pltpu.VMEM((SLOTS, D), BF), pltpu.VMEM((SLOTS, D), BF), pltpu.VMEM((NDEV, 8, 128), F32)]
+    scr += [DMA((k,)) for k in (NF,) * 4] + [DMA((n, 2)), DMA((n, 2))] + [DMA((k,)) for k in (NB, NB, HT, HT)]
+    scr += [DMA((2, 4)), DMA((2,)), DMA((2,)), DMA((4,)), DMA((NDEV - 1,)), DMA((NDEV - 1,)), DMA((NF, 2))]
+    shapes = ((SHARD, D), (GU, FF), (GU, FF), (GD, D), (8, 128))
     return pl.pallas_call(
-        last_kernel, in_specs=[ANY, ANY, ANY, VMEM, ANY, ANY, VMEM], out_specs=[ANY, VMEM, VMEM, VMEM, ANY],
-        out_shape=[jax.ShapeDtypeStruct((SHARD, D), F32), jax.ShapeDtypeStruct((GU_ROWS, FF2), F32),
-                   jax.ShapeDtypeStruct((GD_ROWS, D), F32), jax.ShapeDtypeStruct((8, 128), F32),
-                   jax.ShapeDtypeStruct((HALF, D), F32)],
-        scratch_shapes=scr, compiler_params=params(7, 63), name='last_sums')(d_down, d_gu, dxs, rows, g_all, hn_all, loss8)
-
-
-def rms_inv(values):
-    return lax.rsqrt(jnp.mean(values * values, axis=-1, keepdims=True) + NORM_EPS)
-
-
-def rms_backward(values, inv_rms, gain_vec, grad_out):
-    scaled = grad_out * gain_vec
-    return inv_rms * scaled - values * (inv_rms ** 3) * jnp.mean(scaled * values, axis=-1, keepdims=True)
-
-
-FT = 768
-FT2 = 2 * FT
-NF = FF // FT
+        last_kernel, in_specs=[ANY] * 10 + [VMEM] * 6, out_specs=[ANY] * 4 + [VMEM] * 2 + [ANY],
+        out_shape=[jax.ShapeDtypeStruct(shape, F32) for shape in shapes] + [
+            jax.ShapeDtypeStruct((TOK, D), BF), jax.ShapeDtypeStruct((HALF, D), F32)],
+        scratch_shapes=scr, compiler_params=params(7, 63), name='last_sums')(*args)
 
 
 def mlp_fwd_kernel(x_ref, gm_ref, gf_ref, wgu_ref, wd_ref, a_ref, gu_ref, q_ref, h_ref, hn_ref, acc):
@@ -622,53 +725,6 @@
         compiler_params=pltpu.CompilerParams(vmem_limit_bytes=40 * 2 ** 20), name='mlp_fwd')(x, gain_mlp, gain_final, w_gu, w_down)
 
 
-def mlp_bwd_kernel(dh_ref, h_ref, x_ref, a_ref, gu_ref, q_ref, gm_ref, gf_ref, slot_ref, wgu_ref, wd_ref,
-                   dd_ref, dgu_ref, dx_ref, dxs_ref, dh_s, dm_s, dn):
-    f = pl.program_id(0)
-
-    @pl.when(f == 0)
-    def _():
-        h = h_ref[...].astype(F32)
-        dh = rms_backward(h, rms_inv(h), gf_ref[...], dh_ref[...])
-        dh_s[...] = dh
-        dm_s[...] = dh.astype(BF)
-        dn[...] = jnp.zeros_like(dn)
-    dm = dm_s[...]
-    dd_ref[...] = dot_first(q_ref[...], dm)
-    dq = dot_last(dm, wd_ref[...])
-    g, u = gu_ref[:, :FT].astype(F32), gu_ref[:, FT:].astype(F32)
-    sig = jax.nn.sigmoid(g)
-    dg = (dq * u * sig * (1.0 + g * (1.0 - sig))).astype(BF)
-    du = (dq * g * sig).astype(BF)
-    a = a_ref[...]
-    dgu_ref[:, :FT] = dot_first(a, dg)
-    dgu_ref[:, FT:] = dot_first(a, du)
-    dn[...] += dot_last(dg, wgu_ref[:, :FT]) + dot_last(du, wgu_ref[:, FT:])
-
-    @pl.when(f == NF - 1)
-    def _():
-        x = x_ref[...].astype(F32) * EMB_SCALE
-        dx = (dh_s[...] + rms_backward(x, rms_inv(x), gm_ref[...], dn[...])).astype(BF)
-        dx_ref[...] = dx
-        pick = lax.broadcasted_iota(jnp.int32, (SLOTS, TOK), 0) == slot_ref[...]
-        dxs_ref[...] = dot_plain(jnp.where(pick, 1.0, 0.0).astype(BF), dx).astype(BF)
-
-
-def mlp_backward(d_hid, h, x, a, gu, q, gain_mlp, gain_final, slot, w_gu, w_down):
-    return pl.pallas_call(
-        mlp_bwd_kernel, grid=(NF,),
-        in_specs=[whole((TOK, D)), whole((TOK, D)), whole((TOK, D)), whole((TOK, D)), pl.BlockSpec((TOK, FT2), lambda f: (0, f)),
-                  pl.BlockSpec((TOK, FT), lambda f: (0, f)), whole((1, D)), whole((1, D)), whole((1, TOK)),
-                  pl.BlockSpec((D, FT2), lambda f: (0, f)), pl.BlockSpec((FT, D), lambda f: (f, 0))],
-        out_specs=[pl.BlockSpec((FT, D), lambda f: (f, 0)), pl.BlockSpec((D, FT2), lambda f: (0, f)), whole((TOK, D)),
-                   whole((SLOTS, D))],
-        out_shape=[jax.ShapeDtypeStruct((FF, D), F32), jax.ShapeDtypeStruct((D, FF2), F32), jax.ShapeDtypeStruct((TOK, D), BF),
-                   jax.ShapeDtypeStruct((SLOTS, D), BF)],
-        scratch_shapes=[pltpu.VMEM((TOK, D), F32), pltpu.VMEM((TOK, D), BF), pltpu.VMEM((TOK, D), F32)],
-        compiler_params=pltpu.CompilerParams(vmem_limit_bytes=60 * 2 ** 20),
-        name='mlp_bwd')(d_hid, h, x, a, gu, q, gain_mlp, gain_final, slot, w_gu, w_down)
-
-
 def join_parts(gate, up):
     return jnp.concatenate([w[:, f * FT:(f + 1) * FT] for f in range(NF) for w in (gate, up)], 1)
 
@@ -686,6 +742,9 @@
         grp = jnp.take(both, rel, axis=0)
         ids, labs = grp[:, 0], grp[:, 1]
 
+        def mid(v):
+            return jnp.expand_dims(v, 1)
+
         def local_row(v):
             within = v % (CHIP_ROWS)
             row = jnp.where(within // SHARD == core, 0, HALF) + within % SHARD
@@ -694,25 +753,25 @@
         rows = local_row(ids)
         lab_row = local_row(labs)
         mine = (rows >= 0).astype(F32)
-        before = (jnp.arange(TOK)[:, None] < jnp.arange(TOK)[None, :]).astype(F32)
+        before = jnp.triu(jnp.ones((TOK, TOK), F32), 1)
         rank = dot_plain(mine, before).astype(jnp.int32)
-        slots = jnp.arange(CAP, dtype=jnp.int32)
+        slots = jnp.arange(CAP).reshape(CAP, 1)
         own_chip = ids[0] // (CHIP_ROWS)
         own_rel = jnp.bitwise_xor(own_chip, chip)
-        is_rel = own_rel[None, :] == jnp.arange(NB)[:, None]
+        is_rel = own_rel == jnp.arange(NB).reshape(NB, 1)
         own_rank_all = dot_plain(is_rel.astype(F32), before)
         own_rank = jnp.sum(jnp.where(is_rel, own_rank_all, 0.0), 0).astype(jnp.int32)
-        counts = jnp.sum((both[:, 0] // (CHIP_ROWS))[:, None, :] == jnp.arange(NB)[None, :, None], axis=-1)
+        counts = jnp.sum(both[:, :1] // CHIP_ROWS == jnp.arange(NB).reshape(NB, 1), axis=-1)
         rounds = (jnp.max(counts) + CAP - 1) // CAP
 
         def slot_rows(rnd):
-            want = (rows[:, None, :] >= 0) & (rank[:, None, :] - rnd * CAP == slots[None, :, None])
-            got = jnp.sum(jnp.where(want, rows[:, None, :] + 1, 0), axis=-1) - 1
+            row, at = mid(rows), mid(rank)
+            got = jnp.sum(jnp.where((row >= 0) & (at - rnd * CAP == slots), row + 1, 0), axis=-1) - 1
             return got.reshape(SLOTS)
 
         def slot_tokens(rnd):
-            want = is_rel[:, None, :] & (own_rank[None, None, :] - rnd * CAP == slots[None, :, None])
-            return jnp.sum(jnp.where(want, jnp.arange(TOK)[None, None, :], 0), axis=-1).reshape(SLOTS)
+            want = mid(is_rel) & (own_rank - rnd * CAP == slots)
+            return jnp.sum(jnp.where(want, jnp.arange(TOK), 0), axis=-1).reshape(SLOTS)
 
         def lookup(rnd, x, cid):
             out = jnp.take(e_loc, jnp.maximum(slot_rows(rnd), 0), axis=0, mode='clip').reshape(NB, CAP, D)
@@ -732,8 +791,11 @@
         d_hid, g_all, loss8 = head_backward(hn_all, e_loc, lse, lab_pos)
 
         slot = jnp.where(own_rank < CAP, own_rel * CAP + own_rank, -1)[None, :]
-        d_down, d_gu, d_x, dxs = mlp_backward(d_hid, hid, x_bf, normed, gu, hidden_act, gm, gf, slot, w_gu, w_down)
-        d_embed, d_gu, d_down, loss8, _ = last_sums(d_down, d_gu, dxs, slot_rows(0)[None, :], g_all, hn_all, loss8)
+        cols = jnp.arange(D).reshape(NB, 2, GU)
+        perm = jnp.concatenate([jnp.take(cols, k, axis=1).reshape(1, -1) for k in (core, 1 - core)], 1)
+        d_embed, d_gate, d_up, d_down, loss8, d_x, _ = last_sums(
+            d_hid, hid, x_bf, normed, gu, hidden_act, w_gu, w_down, g_all, hn_all,
+            gm, gf, slot, slot_rows(0)[None, :], perm, loss8)
         loss = -jnp.sum(loss8) * (1.0 / TOTAL)
 
         def more(c):
@@ -746,8 +808,7 @@
             return rnd + 1, acc + part[:SHARD] + lax.ppermute(part[HALF:HALF + SHARD], 'fsdp', pairs)
 
         d_embed = lax.while_loop(lambda c: c[0] < rounds, more, (jnp.int32(1), d_embed))[1]
-        d_gu = d_gu.reshape(-1, NF, 2, FT)
-        return loss, d_embed, d_gu[:, :, 0].reshape(-1, FF), d_gu[:, :, 1].reshape(-1, FF), d_down
+        return loss, d_embed, d_gate, d_up, d_down
 
     shard = P('fsdp', None)
     return jax.shard_map(local_step, mesh=mesh, in_specs=(shard,) * 6 + (P(), P()),

time: 530 us -> 520 us (0.981)
  waiting for transfers between devices: 29.9 us -> 23.4 us
  Pallas kernels: 409 us -> 403 us
    pallas_call x2 -> x1, Pallas kernels: 163 us -> 154 us  [last_sums(): pl.pallas_call(last_kernel, in_specs=[ANY] * 10 + [VMEM] * 6, out_specs=[...]
    all_gather x1, waiting for transfers between devices: 29.1 us -> 22.7 us  [local_step(): w_gu = lax.all_gather(join_parts(gate_shard, up_shard), 'fsdp', tiled=True)]
    unnamed x57 -> x69, local copies, waits for them, and re-layouts: 27.1 us -> 33.1 us
  transfers between devices with their start and end apart: 2 -> 2, of which waited for: 1 -> 1; matrix products, arithmetic and copies ran while one was open for 4% -> 6% of each run, Pallas kernels for 6% -> 7%
where the time goes in v4:
time: 520 us; the launch traced here: 510 us
  Pallas kernels  403 us (78%)
  local copies, waits for them, and re-layouts  46 us (9%)
  waiting for transfers between devices  23.4 us (4%)
  between operations  17.5 us (3%)
  blocking collectives  15.1 us (3%)
    pallas_call x1, Pallas kernels, last_sums(): pl.pallas_call(last_kernel, in_specs=[ANY] * 10 + [VMEM] * 6, out_specs=[...  154 us
    pallas_call x1, Pallas kernels, head_backward(): pl.pallas_call(bwd_kernel, in_specs=[ANY, ANY, VMEM, VMEM], out_specs=[VM...  128 us
    pallas_call x1, Pallas kernels, head_forward(): pl.pallas_call(fwd_kernel, in_specs=[ANY, ANY], out_specs=[ANY, VMEM], ou...  71 us
    unnamed x69, local copies, waits for them, and re-layouts  33.1 us
    pallas_call x1, Pallas kernels, swap(): pl.pallas_call(swap_kernel, in_specs=[VMEM], out_specs=VMEM, out_shape=ja...  24.9 us
    all_gather x1, waiting for transfers between devices, local_step(): w_gu = lax.all_gather(join_parts(gate_shard, up_shard), 'fsdp', tiled=True)  22.7 us
    pallas_call x1, Pallas kernels, mlp_forward(): pl.pallas_call(mlp_fwd_kernel, grid=(NF,), in_specs=[whole((TOK, D)), who...  15.5 us
    all_gather x1, blocking collectives, local_step(): both = lax.all_gather(jnp.concatenate([ids_blk, lab_blk]), 'fsdp')  15.1 us
  transfers between devices with their start and end apart: 2, of which 1 were waited for; matrix products, arithmetic and copies ran while one was open for 6% of the time, Pallas kernels for 7%

profile of v4, /device:TPU:0, one launch (start us, length us, event | category | flops | bytes accessed | tf_op | source)
XLA Modules:
  0.0 510.4 jit_solution(8117856043664766412)
XLA Ops:
  7.2 0.7 all-gather.7.cloned.1.call-update
  7.9 0.8 slice_dynamic-update-slice_fusion.15
  8.7 0.8 slice_dynamic-update-slice_fusion.14
  9.5 0.8 slice_dynamic-update-slice_fusion.13
  10.3 0.8 slice_dynamic-update-slice_fusion.12
  11.1 0.8 slice_dynamic-update-slice_fusion.11
  11.8 0.8 slice_dynamic-update-slice_fusion.10
  12.6 0.8 slice_dynamic-update-slice_fusion.9
  13.4 0.8 slice_dynamic-update-slice_fusion.8
  14.2 0.8 slice_dynamic-update-slice_fusion.7
  15.0 0.8 slice_dynamic-update-slice_fusion.6
  15.7 0.8 slice_dynamic-update-slice_fusion.5
  16.5 0.8 slice_dynamic-update-slice_fusion.4
  17.3 0.8 slice_dynamic-update-slice_fusion.3
  18.1 0.8 slice_dynamic-update-slice_fusion.2
  18.8 0.8 slice_dynamic-update-slice_fusion.1
  19.6 0.8 slice_dynamic-update-slice_fusion
  20.4 0.8 copy-done.9
  21.3 0.7 add_bitcast_fusion.1
  22.0 15.1 %all-gather.1 = s32[16,2,512]{2,1,0:T(2,128)S(1)} all-gather(s32[1,2,512]{2,1,0:T(2,128)S(1)} %add_bitcast_fusion.1), channel_id=2, replica_groups=mesh['fsdp'=16] {'fsdp'}, dimensions={0}, use_global_device_ids=true | all-gather | bytes 69632 | tf_op jit(solution)/shard_map/all_gather | solution.py:736
  37.7 0.6 reduce_max.9
  39.2 0.6 gather_fusion.3
  40.3 0.4 select_reduce_fusion.3
  40.9 2.4 copy-done.1
  43.2 9.8 %pair_gather.1.e_ref = bf16[6400,768]{1,0:T(8,128)(2,1)} custom-call(bf16[3144,768]{1,0:T(8,128)(2,1)S(1)} %copy-done.1), custom_call_target="tpu_custom_call" | custom-call | tf_op jit(solution)/shard_map/pair_gather/pallas_call | solution.py:137
  53.4 8.4 %gather_fusion.4 = bf16[768,768]{1,0:T(8,128)(2,1)S(1)} fusion(bf16[6400,768]{1,0:T(8,128)(2,1)} %pair_gather.1.e_ref, s32[1024]{0:T(1024)S(1)} %get-tuple-element.455), kind=kCustom, calls=%fused_computation.4 | custom fusion | bytes 2362368 | tf_op jit(solution)/shard_map/jit(_take)/gather | solution.py:777
  61.8 24.9 %swap.10 = bf16[8,96,768]{2,1,0:T(8,128)(2,1)S(1)} custom-call(bf16[8,96,768]{2,1,0:T(8,128)(2,1)S(1)} %bitcast.149), custom_call_target="tpu_custom_call" | custom-call | tf_op jit(solution)/shard_map/swap/pallas_call | solution.py:158
  86.8 0.7 sub.186.rows_ref
  87.6 2.0 gather_fusion.5
  90.0 0.6 pad_add_fusion.perm_ref
  90.6 0.6 compare_select_fusion.1.slot_ref
  91.3 0.5 while.28
  91.9 22.7 %all-gather.5.cloned.1.call-done.wgu_ref = bf16[768,6144]{1,0:T(8,128)(2,1)} async-done(((bf16[48,6144]{1,0:T(8,128)(2,1)}), bf16[768,6144]{1,0:T(8,128)(2,1)}) %all-gather.5.cloned.1.call-update) | async-done | bytes 9437200 | tf_op jit(solution)/shard_map/all_gather | solution.py:737
  114.5 2.3 copy-done
  116.9 15.5 %mlp_fwd.1 = (bf16[512,768]{1,0:T(8,128)(2,1)S(1)}, bf16[512,6144]{1,0:T(8,128)(2,1)}, bf16[512,3072]{1,0:T(8,128)(2,1)S(1)}, bf16[512,768]{1,0:T(8,128)(2,1)S(1)}, bf16[512,768]{1,0:T(8,128)(2,1)S(1)}) custom-call(bf16[512,768]{1,0:T(8,128)(2,1)S(1)} %get-tuple-element.311.x_ref, f32[1,768]{1,0:T(1,128)S(1)} %broadcast_in_dim.201.gm_ref, ...), custom_call_target="tpu_custom_call" | custom-call | tf_op jit(solution)/shard_map/mlp_fwd/pallas_call | solution.py:717
  132.4 1.6 copy-done.2
  134.0 0.9 copy-done.3
  134.9 0.9 copy-done.4
  135.8 0.9 copy-done.5
  136.7 71.0 %head_fwd.1 = (bf16[4096,768]{1,0:T(8,128)(2,1)}, f32[8,1,512]{2,1,0:T(1,128)}) custom-call(bf16[512,768]{1,0:T(8,128)(2,1)} %copy-done.5, bf16[6400,768]{1,0:T(8,128)(2,1)} %get-tuple-element.659), custom_call_target="tpu_custom_call" | custom-call | tf_op jit(solution)/shard_map/head_fwd/pallas_call | solution.py:274
  207.8 127.7 %head_bwd.1 = (f32[512,768]{1,0:T(8,128)}, bf16[6400,4096]{1,0:T(8,128)(2,1)}, f32[8,512]{1,0:T(8,128)}) custom-call(bf16[4096,768]{1,0:T(8,128)(2,1)} %get-tuple-element.313.hn_ref, bf16[6400,768]{1,0:T(8,128)(2,1)} %get-tuple-element.659, f32[8,1,512]{2,1,0:T(1,128)} %get-tuple-element.314.lse_ref, s32[8,1,512]{2,1,0:T(1,128)} %bitcast.158), custom_call_target="tpu_custom_call" | custom-call | tf_op jit(solution)/shard_map/head_bwd/pallas_call | solution.py:377
  335.5 153.9 %last_sums.1 = (f32[3144,768]{1,0:T(8,128)}, f32[48,3072]{1,0:T(8,128)}, f32[48,3072]{1,0:T(8,128)}, f32[192,768]{1,0:T(8,128)}, f32[8,128]{1,0:T(8,128)}, /*ind...) custom-call(f32[512,768]{1,0:T(8,128)} %get-tuple-element.315.dhid_ref, bf16[512,768]{1,0:T(8,128)(2,1)} %copy-done.4, ...), custom_call_target="tpu_custom_call" | custom-call | tf_op jit(solution)/shard_map/last_sums/pallas_call | solution.py:680
  489.4 0.7 copy-done.16
  490.1 0.6 reduce_sum.80
  491.3 8.3 %copy.96 = f32[3144,768]{1,0:T(8,128)} copy(f32[3144,768]{1,0:T(8,128)} %get-tuple-element.652) | data formatting | bytes 19316736
  499.6 0.8 copy.97
  500.4 0.8 copy.98
  501.2 0.8 copy.99
  (82 shorter events, 2.2 us)
Async XLA Ops:
  7.2 84.7 %all-gather.7.cloned.1.call-start = ((), (), s32[]{:S(2)}) async-start(), calls=%async_computation.1 | async-start | bytes 5013504 | tf_op jit(solution)/shard_map/all_gather | solution.py:738
  7.9 106.6 %all-gather.5.cloned.1.call-start = ((), (), s32[]{:S(2)}) async-start(), calls=%async_computation | async-start | bytes 10027008 | tf_op jit(solution)/shard_map/all_gather | solution.py:737
  20.4 0.8 copy-start.9
  40.9 2.4 copy-start.1
  61.8 25.0 %copy-start.14 = (f32[768]{0:T(1024)S(1)}, f32[768]{0:T(1024)}, u32[]{:S(2)}) copy-start(f32[768]{0:T(1024)} %param.20) | copy-start | bytes 9220
  61.8 25.0 %copy-start.15 = (f32[768]{0:T(1024)S(1)}, f32[768]{0:T(1024)}, u32[]{:S(2)}) copy-start(f32[768]{0:T(1024)} %param.21) | copy-start | bytes 9220
  86.8 27.8 %copy-start.6 = (f32[1,768]{1,0:T(1,128)}, f32[1,768]{1,0:T(1,128)S(1)}, u32[]{:S(2)}) copy-start(f32[1,768]{1,0:T(1,128)S(1)} %broadcast_in_dim.201.gm_ref) | copy-start | bytes 9220
  86.8 27.7 %copy-start.7 = (f32[1,768]{1,0:T(1,128)}, f32[1,768]{1,0:T(1,128)S(1)}, u32[]{:S(2)}) copy-start(f32[1,768]{1,0:T(1,128)S(1)} %broadcast_in_dim.202.gf_ref) | copy-start | bytes 9220
  90.0 1.4 copy-start.13
  91.8 40.5 %copy-start.8 = (bf16[512,768]{1,0:T(8,128)(2,1)}, bf16[512,768]{1,0:T(8,128)(2,1)S(1)}, u32[]{:S(2)}) copy-start(bf16[512,768]{1,0:T(8,128)(2,1)S(1)} %get-tuple-element.311.x_ref) | copy-start | bytes 2359300
  114.5 2.3 copy-start
  132.4 1.6 copy-start.2
  134.0 0.9 copy-start.3
  134.9 0.9 copy-start.4
  135.8 0.9 copy-start.5
  489.4 0.7 copy-start.16
  491.3 8.3 %copy-start.12 = (f32[48,3072]{1,0:T(8,128)S(1)}, f32[48,3072]{1,0:T(8,128)}, u32[]{:S(2)}) copy-start(f32[48,3072]{1,0:T(8,128)} %get-tuple-element.653) | copy-start | bytes 1769476
  491.3 9.1 %copy-start.11 = (f32[48,3072]{1,0:T(8,128)S(1)}, f32[48,3072]{1,0:T(8,128)}, u32[]{:S(2)}) copy-start(f32[48,3072]{1,0:T(8,128)} %get-tuple-element.654) | copy-start | bytes 1769476
  499.6 1.6 copy-start.10
Sparse Core Ops, SparseCore 0:
  10.2 40.3 all-gather.6
  53.4 61.1 all-gather.4
